TPU v7x, 32 devices: a 4x4x1 block of a 4x4x8 slice. The times are simulated.
32 devices in a mesh: dp: 1 (over z), tp: 4 (over y), ep: 8 (over x, core).
Axes of the slice: x: 4, y: 4, z: 1, core: 2. Of those that a mesh axis runs over, the one named last changes fastest.
The devices are a block of a 4x4x8 slice.
Arguments:
- tokens: bfloat16 [8192, 1536], P(('dp', 'ep', 'tp'))
- expert_ids: int32 [8192, 8], P(('dp', 'ep', 'tp'))
- gate_vals: float32 [8192, 8], P(('dp', 'ep', 'tp'))
- w_one: bfloat16 [40, 1536, 512], P('ep', None, 'tp')
- w_three: bfloat16 [40, 1536, 512], P('ep', None, 'tp')
- w_two: bfloat16 [40, 512, 1536], P('ep', 'tp')
- d_out: bfloat16 [8192, 1536], P(('dp', 'ep', 'tp'))
Outputs:
- output 1: bfloat16 [8192, 1536], P(('dp', 'ep', 'tp'))
- output 2: bfloat16 [8192, 1536], P(('dp', 'ep', 'tp'))
- output 3: bfloat16 [40, 1536, 512], P(('dp', 'ep'), None, 'tp')
- output 4: bfloat16 [40, 1536, 512], P(('dp', 'ep'), None, 'tp')
- output 5: bfloat16 [40, 512, 1536], P(('dp', 'ep'), 'tp')
All inputs are finite; a program needn't handle non-finite values.
Results may differ from a plain program's by a relative error of at most 0.0104073.
Values are sent between devices in bfloat16 or wider.
A program may use at most 768 MiB of HBM per device.

v0:
```python
import jax
import jax.numpy as jnp
from jax import lax
from jax.sharding import PartitionSpec as P


def slot_count(num_top, tok_dev, experts):
    return 8 * ((5 * num_top * tok_dev + 32 * experts - 1) // (32 * experts))


def route_tables(expert_ids, experts, slot_cap):
    row_count, num_top = expert_ids.shape
    hit_mask = expert_ids[:, :, None] == jnp.arange(experts, dtype=jnp.int32)
    per_row = jnp.sum(hit_mask, axis=1, dtype=jnp.int32)
    before = jnp.cumsum(per_row, axis=0) - per_row
    slot_pos = jnp.sum(jnp.where(hit_mask, before[:, None, :], 0), axis=2)
    copy_slot = jnp.where(slot_pos < slot_cap, expert_ids * slot_cap + slot_pos, experts * slot_cap)
    slot_copy = jnp.full((experts * slot_cap,), row_count * num_top, jnp.int32)
    slot_copy = slot_copy.at[copy_slot.reshape(-1)].set(jnp.arange(row_count * num_top, dtype=jnp.int32), mode="drop")
    return slot_copy, copy_slot


def take_rows(source, index_list):
    return jnp.take(source, index_list, axis=0, mode="fill", fill_value=0)


def solution(mesh):
    ep_size = mesh.shape["ep"]
    row_spec = P(("dp", "ep", "tp"), None)
    col_spec = P("ep", None, "tp")
    down_spec = P("ep", "tp", None)
    grad_col = P(("dp", "ep"), None, "tp")
    grad_down = P(("dp", "ep"), "tp", None)

    def local_step(tokens, expert_ids, gate_vals, w_one, w_three, w_two, d_out):
        tok_dev, model_width = tokens.shape
        num_top = expert_ids.shape[1]
        experts = w_one.shape[0] * ep_size
        slot_cap = slot_count(num_top, tok_dev, experts)
        slot_copy, copy_slot = route_tables(expert_ids, experts, slot_cap)
        slot_in = take_rows(tokens, slot_copy // num_top).reshape(experts, slot_cap, model_width)
        recv_in = lax.all_to_all(slot_in, "ep", 0, 1, tiled=True)
        rows_in = lax.all_gather(recv_in, "tp", axis=1, tiled=True)
        act_one = jnp.einsum("end,edf->enf", rows_in, w_one, preferred_element_type=jnp.float32)
        act_three = jnp.einsum("end,edf->enf", rows_in, w_three, preferred_element_type=jnp.float32)
        sig_one = jax.nn.sigmoid(act_one)
        silu_one = act_one * sig_one
        hidden = (silu_one * act_three).astype(jnp.bfloat16)
        part_out = jnp.einsum("enf,efd->end", hidden, w_two, preferred_element_type=jnp.float32)
        mine_out = lax.psum_scatter(part_out, "tp", scatter_dimension=1, tiled=True).astype(jnp.bfloat16)
        back_out = lax.all_to_all(mine_out, "ep", 1, 0, tiled=True).reshape(experts * slot_cap, model_width)
        out_copies = take_rows(back_out, copy_slot)
        out_rows = jnp.sum(gate_vals[:, :, None] * out_copies.astype(jnp.float32), axis=1).astype(jnp.bfloat16)

        grad_copies = (gate_vals[:, :, None] * d_out.astype(jnp.float32)[:, None, :]).astype(jnp.bfloat16)
        slot_grad = take_rows(grad_copies.reshape(tok_dev * num_top, model_width), slot_copy).reshape(experts, slot_cap, model_width)
        recv_grad = lax.all_to_all(slot_grad, "ep", 0, 1, tiled=True)
        rows_grad = lax.all_gather(recv_grad, "tp", axis=1, tiled=True)
        d_hidden = jnp.einsum("end,efd->enf", rows_grad, w_two, preferred_element_type=jnp.float32)
        grad_two = jnp.einsum("enf,end->efd", hidden, rows_grad, preferred_element_type=jnp.float32).astype(jnp.bfloat16)
        d_one = (d_hidden * act_three * sig_one * (1.0 + act_one * (1.0 - sig_one))).astype(jnp.bfloat16)
        d_three = (d_hidden * silu_one).astype(jnp.bfloat16)
        grad_one = jnp.einsum("end,enf->edf", rows_in, d_one, preferred_element_type=jnp.float32).astype(jnp.bfloat16)
        grad_three = jnp.einsum("end,enf->edf", rows_in, d_three, preferred_element_type=jnp.float32).astype(jnp.bfloat16)
        part_dx = jnp.einsum("enf,edf->end", d_one, w_one, preferred_element_type=jnp.float32) + jnp.einsum("enf,edf->end", d_three, w_three, preferred_element_type=jnp.float32)
        mine_dx = lax.psum_scatter(part_dx, "tp", scatter_dimension=1, tiled=True).astype(jnp.bfloat16)
        back_dx = lax.all_to_all(mine_dx, "ep", 1, 0, tiled=True).reshape(experts * slot_cap, model_width)
        dx_rows = jnp.sum(take_rows(back_dx, copy_slot).astype(jnp.float32), axis=1).astype(jnp.bfloat16)
        return out_rows, dx_rows, grad_one, grad_three, grad_two

    return jax.shard_map(local_step, mesh=mesh,
                         in_specs=(row_spec, row_spec, row_spec, col_spec, col_spec, down_spec, row_spec),
                         out_specs=(row_spec, row_spec, grad_col, grad_col, grad_down), check_vma=False)
```

profile of v0, /device:TPU:97, one launch (start us, length us, event | category | flops | bytes accessed | tf_op | source)
XLA Modules:
  0.0 2044.2 jit_solution(8983177879235361069)
XLA Ops:
  7.3 0.9 convert_reduce_fusion
  8.2 0.6 reduce-window.6
  8.8 0.2 slice_reduce_fusion
  9.1 0.8 select_reduce_fusion
  9.9 1.3 compare_and_fusion.2
  11.2 0.1 copy.63
  11.5 8.1 scatter_custom_fusion
  19.7 9.5 gather_fusion
  29.2 7.0 broadcast_select_fusion.1
  36.2 93.8 %all_to_all.66 = bf16[40,64,1536]{2,1,0:T(8,128)(2,1)S(1)} all-to-all(bf16[40,64,1536]{2,1,0:T(8,128)(2,1)} %broadcast_select_fusion.1), channel_id=1, replica_groups=mesh['dp'=1,'tp'=4,'ep'=8] {'ep'}, dimensions={0} | all-to-all | bytes 15728640 | tf_op jit(solution)/shard_map/all_to_all | solution.py:42
  130.0 3.6 copy.64
  133.8 0.5 copy-done.11
  134.5 0.2 copy-done.8
  134.7 0.2 convert_element_type.47
  134.9 3.9 fusion
  138.8 20.0 gather_fusion.1
  158.8 7.0 broadcast_select_fusion
  165.7 92.7 %all_to_all.67 = bf16[40,64,1536]{2,1,0:T(8,128)(2,1)S(1)} all-to-all(bf16[40,64,1536]{2,1,0:T(8,128)(2,1)} %broadcast_select_fusion), channel_id=1, replica_groups=mesh['dp'=1,'tp'=4,'ep'=8] {'ep'}, dimensions={0} | all-to-all | bytes 15728640 | tf_op jit(solution)/shard_map/all_to_all | solution.py:57
  258.5 3.7 copy.70
  262.2 0.3 reduce-scatter.5.cloned.1.call-start
  262.5 146.4 %all-gather.3.cloned.1.call-done = bf16[5,2048,1536]{2,1,0:T(8,128)(2,1)} async-done(((bf16[5,512,1536]{2,1,0:T(8,128)(2,1)}), bf16[5,2048,1536]{2,1,0:T(8,128)(2,1)}) %all-gather.3.cloned.1.call-update) | async-done | bytes 31457296 | tf_op jit(solution)/shard_map/all_gather | solution.py:43
  408.8 16.3 fusion.9
  425.2 16.1 fusion.8
  441.3 243.5 %all-gather.5.cloned.1.call-done = bf16[5,2048,1536]{2,1,0:T(8,128)(2,1)} async-done(((bf16[5,512,1536]{2,1,0:T(8,128)(2,1)}), bf16[5,2048,1536]{2,1,0:T(8,128)(2,1)}) %all-gather.5.cloned.1.call-update) | async-done | bytes 31457296 | tf_op jit(solution)/shard_map/all_gather | solution.py:58
  684.8 20.0 multiply_convert_fusion
  704.8 24.5 %fusion.11 = f32[5,2048,1536]{2,1,0:T(8,128)} fusion(bf16[5,2048,128]{2,1,0:T(8,128)(2,1)} %get-tuple-element.11, bf16[5,1536,128]{2,1,0:T(8,128)(2,1)} %param.12), kind=kOutput, calls=%fused_computation.53 | convolution fusion | flops 4026531840 | bytes 67502080 | tf_op jit(solution)/shard_map/enf,edf->end/dot_general | solution.py:65
  729.3 45.3 %convolution_add_fusion = f32[5,2048,1536]{2,1,0:T(8,128)} fusion(f32[5,2048,1536]{2,1,0:T(8,128)} %fusion.11, bf16[5,2048,128]{2,1,0:T(8,128)(2,1)} %get-tuple-element.10, bf16[5,1536,128]{2,1,0:T(8,128)(2,1)} %param.13), kind=kOutput, calls=%fused_computation.5 | convolution fusion | flops 4042260480 | bytes 130416640 | tf_op jit(solution)/shard_map/enf,edf->end/dot_general | solution.py:65
  774.8 24.3 %fusion.10 = f32[5,2048,1536]{2,1,0:T(8,128)} fusion(bf16[5,2048,128]{2,1,0:T(8,128)(2,1)} %get-tuple-element.12, bf16[5,128,1536]{2,1,0:T(8,128)(2,1)S(1)} %copy-done), kind=kOutput, calls=%fused_computation.52 | convolution fusion | flops 4026531840 | bytes 67502080 | tf_op jit(solution)/shard_map/enf,efd->end/dot_general | solution.py:49
  799.2 492.9 %reduce-scatter.5.cloned.1.call-done = f32[5,512,1536]{2,1,0:T(8,128)} async-done(((f32[5,2048,1536]{2,1,0:T(8,128)}), f32[5,512,1536]{2,1,0:T(8,128)}) %reduce-scatter.5.cloned.1.call-update) | async-done | bytes 15728656 | tf_op jit(solution)/shard_map/reduce_scatter | solution.py:66
  1292.0 9.5 convert_element_type.51
  1301.5 11.9 copy.71
  1313.5 6.2 all-to-all-start.3
  1319.7 491.0 %reduce-scatter.3.cloned.1.call-done = f32[5,512,1536]{2,1,0:T(8,128)} async-done(((f32[5,2048,1536]{2,1,0:T(8,128)}), f32[5,512,1536]{2,1,0:T(8,128)}) %reduce-scatter.3.cloned.1.call-update) | async-done | bytes 15728656 | tf_op jit(solution)/shard_map/reduce_scatter | solution.py:50
  1810.7 9.5 convert_element_type.44
  1820.2 12.0 copy.65
  1832.2 6.6 all-to-all-start.1
  1838.9 0.2 copy.62
  1839.0 0.1 copy.67
  1839.3 16.4 convolution_convert_fusion
  1855.7 16.9 convolution_convert_fusion.1
  1872.6 17.6 convolution_convert_fusion.2
  1890.2 10.9 copy.72
  1901.1 76.2 %all-to-all-done.1 = bf16[5,512,1536]{2,0,1:T(8,128)(2,1)} async-done(((bf16[5,512,1536]{2,0,1:T(8,128)(2,1)}), bf16[5,512,1536]{2,0,1:T(8,128)(2,1)}, u32[]{:S(2)}, u32[]{:S(2)}) %all-to-all-start.1) | async-done | bytes 7864352 | tf_op jit(solution)/shard_map/all_to_all | solution.py:51
  1977.3 11.0 copy.66
  1988.2 17.5 gather_fusion.3
  2005.7 17.9 gather_fusion.2
  2023.7 7.0 fusion.1
  2030.7 6.5 multiply_reduce_fusion
  (50 shorter events, 1.3 us)
Async XLA Ops:
  7.2 677.6 %copy-start = (bf16[5,128,1536]{2,1,0:T(8,128)(2,1)S(1)}, bf16[5,128,1536]{2,1,0:T(8,128)(2,1)}, u32[]{:S(2)}) copy-start(bf16[5,128,1536]{2,1,0:T(8,128)(2,1)} %param.14) | copy-start | bytes 5898244
  7.2 12.5 copy-start.2
  7.2 401.6 %all-gather.3.cloned.1.call-start = ((), (), s32[]{:S(2)}) async-start(), calls=%async_computation.6 | async-start | bytes 39321600 | tf_op jit(solution)/shard_map/all_gather | solution.py:43
  11.2 18.0 copy-start.9
  133.6 0.7 copy-start.11
  133.6 1.1 copy-start.8
  133.6 551.1 %all-gather.5.cloned.1.call-start = ((), (), s32[]{:S(2)}) async-start(), calls=%async_computation.8 | async-start | bytes 39321600 | tf_op jit(solution)/shard_map/all_gather | solution.py:58
  134.4 24.4 %copy-start.6 = (f32[256,8]{1,0:T(8,128)}, f32[256,8]{1,0:T(8,128)S(1)}, u32[]{:S(2)}) copy-start(f32[256,8]{1,0:T(8,128)S(1)} %copy.59) | copy-start | bytes 24580
  262.2 1029.8 %reduce-scatter.5.cloned.1.call-start = ((), (), s32[]{:S(2)}) async-start(), calls=%async_computation.9 | async-start | bytes 78643200 | tf_op jit(solution)/shard_map/reduce_scatter | solution.py:66
  408.8 16.3 copy-start.5
  774.7 1036.0 %reduce-scatter.3.cloned.1.call-start = ((), (), s32[]{:S(2)}) async-start(), calls=%async_computation.7 | async-start | bytes 78643200 | tf_op jit(solution)/shard_map/reduce_scatter | solution.py:50
  1313.5 518.7 %all-to-all-start.3 = ((bf16[5,512,1536]{2,0,1:T(8,128)(2,1)}), bf16[5,512,1536]{2,0,1:T(8,128)(2,1)}, u32[]{:S(2)}, u32[]{:S(2)}) async-start(bf16[5,512,1536]{2,0,1:T(8,128)(2,1)} %copy.71), calls=%async_computation.5 | async-start | bytes 25165824 | tf_op jit(solution)/shard_map/all_to_all | solution.py:67
  1832.2 6.7 copy-start.12
  1832.2 6.8 copy-start.10
  1832.2 145.1 %all-to-all-start.1 = ((bf16[5,512,1536]{2,0,1:T(8,128)(2,1)}), bf16[5,512,1536]{2,0,1:T(8,128)(2,1)}, u32[]{:S(2)}, u32[]{:S(2)}) async-start(bf16[5,512,1536]{2,0,1:T(8,128)(2,1)} %copy.65), calls=%async_computation.2 | async-start | bytes 25165824 | tf_op jit(solution)/shard_map/all_to_all | solution.py:51
  1855.7 16.9 copy-start.4
  2005.7 31.5 %copy-start.1 = (bf16[5,128,1536]{2,1,0:T(8,128)(2,1)S(1)}, bf16[5,128,1536]{2,1,0:T(8,128)(2,1)}, u32[]{:S(2)}) copy-start(bf16[5,128,1536]{2,1,0:T(8,128)(2,1)} %param.14) | copy-start | bytes 5898244
  2023.6 7.0 copy-start.3
  2023.7 7.0 copy-start.7
Sparse Core Ops, SparseCore 0:
  133.8 275.0 all-gather.2
  410.4 274.2 all-gather.4
  774.8 517.1 reduce-scatter.4
  1294.2 516.3 reduce-scatter.2
where the time goes:
time: 2050 us; the launch traced here: 2040 us
  waiting for transfers between devices  1450 us (71%)
  matrix products  198 us (10%)
  blocking collectives  187 us (9%)
  local copies, waits for them, and re-layouts  128 us (6%)
  other arithmetic  54.4 us (3%)
    reduce_scatter x1, waiting for transfers between devices, local_step(): lax.psum_scatter(part_dx, 'tp', scatter_dimension=1, tiled=True)  493 us
    reduce_scatter x1, waiting for transfers between devices, local_step(): lax.psum_scatter(part_out, 'tp', scatter_dimension=1, tiled=True)  491 us
    all_gather x1, waiting for transfers between devices, local_step(): rows_grad = lax.all_gather(recv_grad, 'tp', axis=1, tiled=True)  243 us
    all_gather x1, waiting for transfers between devices, local_step(): rows_in = lax.all_gather(recv_in, 'tp', axis=1, tiled=True)  146 us
    all_to_all x1, blocking collectives, local_step(): recv_in = lax.all_to_all(slot_in, 'ep', 0, 1, tiled=True)  93.8 us
    all_to_all x1, blocking collectives, local_step(): recv_grad = lax.all_to_all(slot_grad, 'ep', 0, 1, tiled=True)  92.7 us
    all_to_all x1, waiting for transfers between devices, local_step(): lax.all_to_all(mine_out, 'ep', 1, 0, tiled=True)  76.2 us
    gather x4, local copies, waits for them, and re-layouts, take_rows(): return jnp.take(source, index_list, axis=0, mode='fill', fill_value=0)  64.9 us
  transfers between devices with their start and end apart: 6, of which 5 were waited for; matrix products, arithmetic and copies ran while one was open for 10% of the time, Pallas kernels for 0%

commit v1 on v0

v1 whole, which is shorter than its diff:
```python
import functools

import jax
import jax.numpy as jnp
from jax import lax
from jax.experimental import pallas as pl
from jax.experimental.pallas import tpu as pltpu
from jax.sharding import PartitionSpec as P

BF16 = jnp.bfloat16
F32 = jnp.float32


def slot_count(num_top, tok_dev, experts):
    return 8 * ((5 * num_top * tok_dev + 32 * experts - 1) // (32 * experts))


def dot(a, b):
    return jnp.dot(a, b, preferred_element_type=F32)


def dot_tb(a, b):
    return lax.dot_general(a, b, (((1,), (1,)), ((), ())), preferred_element_type=F32)


def dot_ta(a, b):
    return lax.dot_general(a, b, (((0,), (0,)), ((), ())), preferred_element_type=F32)


def block_tables(expert_ids, gate_vals, experts, groups):
    rows = expert_ids.shape[0]
    hit = expert_ids[:, :, None] == jnp.arange(experts, dtype=jnp.int32)
    gate = jnp.sum(jnp.where(hit, gate_vals[:, :, None], 0.0), axis=1)
    routed = jnp.any(hit, axis=1)
    earlier = jnp.arange(rows)[None, :] < jnp.arange(rows)[:, None]
    before = dot(earlier.astype(BF16), routed.astype(BF16))
    pos = jnp.where(routed, before, -1.0)
    own = experts // groups
    table = jnp.stack([pos.T.reshape(groups, own, rows), gate.T.reshape(groups, own, rows)], axis=1)
    return table.reshape(groups * 2 * own, rows)


def hit_masks(table, own, cap):
    slot = lax.broadcasted_iota(jnp.int32, (cap, table.shape[1]), 0).astype(F32)
    return [table[e : e + 1, :] == slot for e in range(own)]


def one_hot(masks):
    return jnp.concatenate([jnp.where(m, 1.0, 0.0) for m in masks], axis=0).astype(BF16)


def slot_gates(masks, table, own):
    return jnp.concatenate([jnp.where(m, table[own + e : own + e + 1, :], 0.0) for e, m in enumerate(masks)], axis=0)


def three_parts(x):
    hi = x.astype(BF16)
    rest = x - hi.astype(F32)
    mid = rest.astype(BF16)
    return hi, mid, (rest - mid.astype(F32)).astype(BF16)


def wgrad_kernel(own, cap, width, tab, x, dy, w13, w2, g1, g3, g2, xs, us, acc13, acc2):
    step = pl.program_id(0)
    blocks = x.shape[1]

    @pl.when(step == 0)
    def _():
        acc13[...] = jnp.zeros_like(acc13)
        acc2[...] = jnp.zeros_like(acc2)

    def gather(b, carry):
        table = tab[0, b]
        masks = hit_masks(table, own, cap)
        pick = one_hot(masks)
        gates = jnp.sum(slot_gates(masks, table, own), axis=1, keepdims=True)
        rows = pl.ds(pl.multiple_of(b * cap, cap), cap)
        picked = dot(pick, x[0, b]).astype(BF16)
        for e in range(own):
            xs[e, rows, :] = picked[e * cap : (e + 1) * cap]
        scaled = (gates * dot(pick, dy[0, b])).astype(BF16)
        for e in range(own):
            us[e, rows, :] = scaled[e * cap : (e + 1) * cap]
        return carry

    lax.fori_loop(0, blocks, gather, 0)

    def expert(e, carry):
        ab = dot(xs[e], w13[e])
        a, b = ab[:, :width], ab[:, width:]
        dh = dot_tb(us[e], w2[e])
        sig = jax.nn.sigmoid(a)
        silu = a * sig
        h = (silu * b).astype(BF16)
        da = (dh * b * sig * (1.0 + a * (1.0 - sig))).astype(BF16)
        db = (dh * silu).astype(BF16)
        acc13[e] += dot_ta(jnp.concatenate([da, db], axis=1), xs[e])
        acc2[e] += dot_ta(h, us[e])
        return carry

    lax.fori_loop(0, own, expert, 0)

    @pl.when(step == pl.num_programs(0) - 1)
    def _():
        def finish(e, carry):
            g1[e] = acc13[e, :width, :].T.astype(BF16)
            g3[e] = acc13[e, width:, :].T.astype(BF16)
            g2[e] = acc2[e].astype(BF16)
            return carry

        lax.fori_loop(0, own, finish, 0)


def weight_grads(table, x_all, dy_all, w13, w2, cap):
    groups, blocks, tok, model = x_all.shape
    own, width = w2.shape[0], w2.shape[1]
    rows = blocks * cap
    whole = lambda *shape: pl.BlockSpec(shape, lambda s: (0,) * len(shape), pipeline_mode=pl.Buffered(1))
    col = jax.ShapeDtypeStruct((own, model, width), BF16)
    slot_rows = groups * rows * own
    return pl.pallas_call(
        functools.partial(wgrad_kernel, own, cap, width),
        grid=(groups,),
        in_specs=[
            pl.BlockSpec((1, blocks, 2 * own, tok), lambda s: (s, 0, 0, 0)),
            pl.BlockSpec((1, blocks, tok, model), lambda s: (s, 0, 0, 0)),
            pl.BlockSpec((1, blocks, tok, model), lambda s: (s, 0, 0, 0)),
            whole(own, model, 2 * width),
            whole(own, width, model),
        ],
        out_specs=[whole(own, model, width), whole(own, model, width), whole(own, width, model)],
        out_shape=[col, col, jax.ShapeDtypeStruct((own, width, model), BF16)],
        scratch_shapes=[
            pltpu.VMEM((own, rows, model), BF16),
            pltpu.VMEM((own, rows, model), BF16),
            pltpu.VMEM((own, 2 * width, model), F32),
            pltpu.VMEM((own, width, model), F32),
        ],
        compiler_params=pltpu.CompilerParams(vmem_limit_bytes=62 * 2**20),
        cost_estimate=pl.CostEstimate(
            flops=2 * slot_rows * model * (2 * tok + 6 * width),
            bytes_accessed=2 * 2 * groups * blocks * tok * model,
            transcendentals=0,
        ),
        name="weight_grads",
    )(table, x_all, dy_all, w13, w2)


def forward_kernel(own, cap, width, where, tab, x, w13, w2, y_out, ab_out, xs, ys):
    step = pl.program_id(0)
    blocks, shards = ys.shape[0], w13.shape[0]

    @pl.when(step < blocks)
    def _():
        pick = one_hot(hit_masks(tab[step, 0], own, cap))
        picked = dot(pick, x[0, 0]).astype(BF16)
        rows = pl.ds(pl.multiple_of(step * cap, cap), cap)
        for e in range(own):
            xs[e, rows, :] = picked[e * cap : (e + 1) * cap]

    @pl.when((step >= blocks) & (step < blocks + own))
    def _():
        e = step - blocks
        parts = []
        for j in range(shards):
            ab = dot(xs[e], w13[j, 0])
            ab_out[0, :, 2 * width * j : 2 * width * (j + 1)] = ab
            a, b = ab[:, :width], ab[:, width:]
            parts.append((a * jax.nn.sigmoid(a) * b).astype(BF16))
        h = jnp.concatenate(parts, axis=1)
        y = dot(h, w2[:, 0].reshape(shards * width, w2.shape[3])).astype(BF16)
        at = pl.ds(pl.multiple_of(e * cap, cap), cap)
        for k in range(blocks):
            ys[k, at, :] = y[k * cap : (k + 1) * cap]

    @pl.when(step >= blocks + own)
    def _():
        k = step - blocks - own
        table = tab[k, 0]
        hi, mid, low = three_parts(slot_gates(hit_masks(table, own, cap), table, own))
        rows = ys[k]
        y_out[0] = dot_ta(hi, rows) + (dot_ta(mid, rows) + dot_ta(low, rows))


def backward_kernel(own, cap, width, where, tab, dy, ab_in, w13, w2, dx_out, us, vs):
    step = pl.program_id(0)
    blocks, shards = vs.shape[0], w13.shape[0]

    @pl.when(step < blocks)
    def _():
        table = tab[step, 0]
        masks = hit_masks(table, own, cap)
        gates = jnp.sum(slot_gates(masks, table, own), axis=1, keepdims=True)
        scaled = (gates * dot(one_hot(masks), dy[0, 0])).astype(BF16)
        rows = pl.ds(pl.multiple_of(step * cap, cap), cap)
        for e in range(own):
            us[e, rows, :] = scaled[e * cap : (e + 1) * cap]

    @pl.when((step >= blocks) & (step < blocks + own))
    def _():
        e = step - blocks
        v = None
        for j in range(shards):
            dh = dot_tb(us[e], w2[j, 0])
            a = ab_in[0, :, 2 * width * j : 2 * width * j + width]
            b = ab_in[0, :, 2 * width * j + width : 2 * width * (j + 1)]
            sig = jax.nn.sigmoid(a)
            da = (dh * b * sig * (1.0 + a * (1.0 - sig))).astype(BF16)
            db = (dh * (a * sig)).astype(BF16)
            part = dot_tb(jnp.concatenate([da, db], axis=1), w13[j, 0])
            v = part if v is None else v + part
        v = v.astype(BF16)
        at = pl.ds(pl.multiple_of(e * cap, cap), cap)
        for k in range(blocks):
            vs[k, at, :] = v[k * cap : (k + 1) * cap]

    @pl.when(step >= blocks + own)
    def _():
        k = step - blocks - own
        pick = one_hot(hit_masks(tab[k, 0], own, cap))
        dx_out[0] = dot_ta(pick, vs[k])


def token_specs(blocks, own, tok, model, width, shards):
    gather = lambda s, w: (jnp.minimum(s, blocks - 1), w[0], 0, 0)
    expert = lambda s: jnp.clip(s - blocks, 0, own - 1)
    return dict(
        tab=pl.BlockSpec((blocks, 1, 2 * own, tok), lambda s, w: (0, w[0], 0, 0)),
        rows=pl.BlockSpec((1, 1, tok, model), gather),
        w13=pl.BlockSpec((shards, 1, model, 2 * width), lambda s, w: (0, expert(s), 0, 0)),
        w2=pl.BlockSpec((shards, 1, width, model), lambda s, w: (0, expert(s), 0, 0)),
        out=pl.BlockSpec((1, tok, model), lambda s, w: (jnp.clip(s - blocks - own, 0, blocks - 1), 0, 0)),
        act=lambda rows: pl.BlockSpec((1, rows, 2 * width * shards), lambda s, w: (expert(s), 0, 0)),
    )


def forward_rows(where, table, x_all, w13_all, w2_all, cap):
    blocks, _, tok, model = x_all.shape
    shards, own, width, _ = w2_all.shape
    rows = blocks * cap
    specs = token_specs(blocks, own, tok, model, width, shards)
    return pl.pallas_call(
        functools.partial(forward_kernel, own, cap, width),
        grid_spec=pltpu.PrefetchScalarGridSpec(
            num_scalar_prefetch=1,
            grid=(2 * blocks + own,),
            in_specs=[specs["tab"], specs["rows"], specs["w13"], specs["w2"]],
            out_specs=[specs["out"], specs["act"](rows)],
            scratch_shapes=[pltpu.VMEM((own, rows, model), BF16), pltpu.VMEM((blocks, own * cap, model), BF16)],
        ),
        out_shape=[
            jax.ShapeDtypeStruct((blocks, tok, model), F32),
            jax.ShapeDtypeStruct((own, rows, 2 * width * shards), F32),
        ],
        compiler_params=pltpu.CompilerParams(vmem_limit_bytes=62 * 2**20),
        cost_estimate=pl.CostEstimate(
            flops=2 * own * rows * model * (4 * tok + 3 * width * shards),
            bytes_accessed=2 * own * 3 * model * width * shards,
            transcendentals=0,
        ),
        name="forward_rows",
    )(where, table, x_all, w13_all, w2_all)


def backward_rows(where, table, dy_all, ab, w13_all, w2_all, cap):
    blocks, _, tok, model = dy_all.shape
    shards, own, width, _ = w2_all.shape
    rows = blocks * cap
    specs = token_specs(blocks, own, tok, model, width, shards)
    return pl.pallas_call(
        functools.partial(backward_kernel, own, cap, width),
        grid_spec=pltpu.PrefetchScalarGridSpec(
            num_scalar_prefetch=1,
            grid=(2 * blocks + own,),
            in_specs=[specs["tab"], specs["rows"], specs["act"](rows), specs["w13"], specs["w2"]],
            out_specs=specs["out"],
            scratch_shapes=[pltpu.VMEM((own, rows, model), BF16), pltpu.VMEM((blocks, own * cap, model), BF16)],
        ),
        out_shape=jax.ShapeDtypeStruct((blocks, tok, model), F32),
        compiler_params=pltpu.CompilerParams(vmem_limit_bytes=62 * 2**20),
        cost_estimate=pl.CostEstimate(
            flops=2 * own * rows * model * (2 * tok + 3 * width * shards),
            bytes_accessed=2 * own * 3 * model * width * shards,
            transcendentals=0,
        ),
        name="backward_rows",
    )(where, table, dy_all, ab, w13_all, w2_all)


def solution(mesh):
    ep_size, tp_size = mesh.shape["ep"], mesh.shape["tp"]
    row_spec = P(("dp", "ep", "tp"), None)
    col_spec = P("ep", None, "tp")
    down_spec = P("ep", "tp", None)
    grad_col = P(("dp", "ep"), None, "tp")
    grad_down = P(("dp", "ep"), "tp", None)

    def local_step(tokens, expert_ids, gate_vals, w_one, w_three, w_two, d_out):
        tok, model = tokens.shape
        own = w_one.shape[0]
        experts = own * ep_size
        cap = slot_count(expert_ids.shape[1], tok, experts)

        def everyone(rows):
            full = lax.all_gather(rows, ("ep", "tp"), axis=0, tiled=True)
            return full.reshape(ep_size, tp_size, rows.shape[0], rows.shape[1])

        w13 = jnp.concatenate([w_one, w_three], axis=2)
        w2_all = lax.all_gather(w_two, "tp", axis=0)
        w13_all = lax.all_gather(w13, "tp", axis=0)

        table = block_tables(expert_ids, gate_vals, experts, ep_size)
        table, w2_all = lax.optimization_barrier((table, w2_all))
        table = everyone(table)
        ep = lax.axis_index("ep")
        table = lax.dynamic_slice_in_dim(table, ep * 2 * own, 2 * own, axis=2)
        where = lax.axis_index("tp").astype(jnp.int32).reshape(1)
        x_all = everyone(tokens)
        dy_all = everyone(d_out)

        y_part, ab = forward_rows(where, table, x_all, w13_all, w2_all, cap)
        out = lax.psum_scatter(y_part, "ep", scatter_dimension=0, tiled=False).astype(BF16)
        dx_part = backward_rows(where, table, dy_all, ab, w13_all, w2_all, cap)
        dx = lax.psum_scatter(dx_part, "ep", scatter_dimension=0, tiled=False).astype(BF16)
        grad_one, grad_three, grad_two = weight_grads(table, x_all, dy_all, w13, w_two, cap)
        return out, dx, grad_one, grad_three, grad_two

    return jax.shard_map(local_step, mesh=mesh,
                         in_specs=(row_spec, row_spec, row_spec, col_spec, col_spec, down_spec, row_spec),
                         out_specs=(row_spec, row_spec, grad_col, grad_col, grad_down), check_vma=False)
```

time: 2050 us -> 607 us (0.30)
  waiting for transfers between devices: 1450 us -> 429 us
  matrix products: 198 us -> 0.17 us
  blocking collectives: 187 us -> 0 us
  Pallas kernels: 0 us -> 150 us
  local copies, waits for them, and re-layouts: 128 us -> 6.42 us
  other arithmetic: 54.4 us -> 6.26 us
    reduce_scatter x2, waiting for transfers between devices: 984 us -> 26.6 us  [the longest x1 26.6 us: local_step(): lax.psum_scatter(dx_part, 'ep', scatter_dimension=0, tiled=False)]
    dot_general x9 -> x1, matrix products: 198 us -> 0.17 us  [dot(): return jnp.dot(a, b, preferred_element_type=F32)]
    all_to_all x2 -> x0, blocking collectives: 187 us -> none  [the longest x1 93.8 us: local_step(): recv_in = lax.all_to_all(slot_in, 'ep', 0, 1, tiled=True)]
    pallas_call x0 -> x3, Pallas kernels: none -> 150 us  [the longest x1 74.5 us: weight_grads(): pl.pallas_call(functools.partial(wgrad_kernel, own, cap, width), grid=(gr...]
    all_to_all x2 -> x0, waiting for transfers between devices: 76.2 us -> none  [the longest x1 76.2 us: local_step(): lax.all_to_all(mine_out, 'ep', 1, 0, tiled=True)]
    gather x4 -> x0, local copies, waits for them, and re-layouts: 64.9 us -> none  [take_rows(): return jnp.take(source, index_list, axis=0, mode='fill', fill_value=0)]
    all_to_all x4 -> x0, local copies, waits for them, and re-layouts: 29.1 us -> none  [the longest x1 11 us: local_step(): lax.all_to_all(mine_out, 'ep', 1, 0, tiled=True)]
    convert_element_type x2 -> x0, local copies, waits for them, and re-layouts: 23.9 us -> none  [the longest x1 12 us: local_step(): lax.psum_scatter(part_out, 'tp', scatter_dimension=1, tiled=True)]
  transfers between devices with their start and end apart: 6 -> 7, of which waited for: 5 -> 6; matrix products, arithmetic and copies ran while one was open for 10% -> 2% of each run, Pallas kernels for 0% -> 25%
where the time goes in v1:
time: 607 us
  waiting for transfers between devices  429 us (71%)
  Pallas kernels  150 us (25%)
  between operations  14.2 us (2%)
  local copies, waits for them, and re-layouts  6.42 us (1%)
  other arithmetic  6.26 us (1%)
    all_gather x3, waiting for transfers between devices, everyone(): full = lax.all_gather(rows, ('ep', 'tp'), axis=0, tiled=True)  179 us
    all_gather x1, waiting for transfers between devices, local_step(): w13_all = lax.all_gather(w13, 'tp', axis=0)  142 us
    all_gather x1, waiting for transfers between devices, local_step(): w2_all = lax.all_gather(w_two, 'tp', axis=0)  79.2 us
    pallas_call x1, Pallas kernels, weight_grads(): pl.pallas_call(functools.partial(wgrad_kernel, own, cap, width), grid=(gr...  74.5 us
    pallas_call x1, Pallas kernels, backward_rows(): pl.pallas_call(functools.partial(backward_kernel, own, cap, width), grid_...  39.1 us
    pallas_call x1, Pallas kernels, forward_rows(): pl.pallas_call(functools.partial(forward_kernel, own, cap, width), grid_s...  36.8 us
    reduce_scatter x1, waiting for transfers between devices, local_step(): lax.psum_scatter(dx_part, 'ep', scatter_dimension=0, tiled=False)  26.6 us
  transfers between devices with their start and end apart: 7, of which 6 were waited for; matrix products, arithmetic and copies ran while one was open for 2% of the time, Pallas kernels for 25%

profile of v1, /device:TPU:97, one launch (start us, length us, event | category | flops | bytes accessed | tf_op | source)
XLA Modules:
  0.0 606.7 jit_solution(6327194820657971293)
XLA Ops:
  7.2 0.0 copy-start
  7.2 0.1 all-gather.14.cloned.1.call-start
  7.3 0.7 all-gather.14.cloned.1.call-update
  8.0 0.1 all-gather.8.cloned.1.call-start
  8.1 0.8 select_reduce_fusion
  8.8 0.7 fusion
  9.6 0.2 convolution_select_fusion
  9.8 0.7 reshape.30
  10.5 79.2 %all-gather.14.cloned.1.call-done = bf16[20,128,1536]{2,1,0:T(8,128)(2,1)} async-done(((bf16[5,128,1536]{2,1,0:T(8,128)(2,1)}), bf16[20,128,1536]{2,1,0:T(8,128)(2,1)}) %all-gather.14.cloned.1.call-update) | async-done | bytes 7864336 | tf_op jit(solution)/shard_map/all_gather | solution.py:309
  89.7 0.1 all-gather.8.cloned.1.call-update
  89.8 0.1 all-gather.16.cloned.1.call-start
  89.8 0.0 copy-done
  89.9 0.0 copy-start.1
  89.9 1.4 constant_dynamic-update-slice_fusion.1
  91.3 0.8 copy-done.1
  92.1 1.5 constant_dynamic-update-slice_fusion.w13
  93.6 0.1 all-gather.16.cloned.1.call-update
  93.6 0.1 all-gather.10.cloned.1.call-start
  93.7 0.6 all-gather.10.cloned.1.call-update
  94.3 0.1 all-gather.12.cloned.1.call-start
  94.3 0.6 all-gather.12.cloned.1.call-update
  94.9 0.1 reduce-scatter.3.cloned.1.call-start
  95.0 37.8 %all-gather.8.cloned.1.call-done = f32[2560,256]{1,0:T(8,128)} async-done(((f32[80,256]{1,0:T(8,128)}), f32[2560,256]{1,0:T(8,128)}) %all-gather.8.cloned.1.call-update) | async-done | bytes 2621456 | tf_op jit(solution)/shard_map/all_gather | solution.py:305
  132.8 2.0 constant_dynamic-slice_fusion.tab
  134.8 141.7 %all-gather.16.cloned.1.call-done = bf16[20,1536,256]{2,1,0:T(8,128)(2,1)} async-done(((bf16[5,1536,256]{2,1,0:T(8,128)(2,1)}), bf16[20,1536,256]{2,1,0:T(8,128)(2,1)}) %all-gather.16.cloned.1.call-update) | async-done | bytes 15728656 | tf_op jit(solution)/shard_map/all_gather | solution.py:310
  276.6 90.3 %all-gather.10.cloned.1.call-done = bf16[8192,1536]{1,0:T(8,128)(2,1)} async-done(((bf16[256,1536]{1,0:T(8,128)(2,1)}), bf16[8192,1536]{1,0:T(8,128)(2,1)}) %all-gather.10.cloned.1.call-update) | async-done | bytes 25165840 | tf_op jit(solution)/shard_map/all_gather | solution.py:305
  366.8 36.8 %forward_rows.1 = (f32[8,256,1536]{2,1,0:T(8,128)}, f32[5,512,1024]{2,1,0:T(8,128)}) custom-call(s32[1]{0:T(128)} %bitcast.where, f32[8,4,10,256]{3,2,1,0:T(8,128)} %constant_dynamic-slice_fusion.tab, bf16[8,4,256,1536]{3,2,1,0:T(8,128)(2,1)} %bitcast.22, bf16[4,5,1536,256]{3,2,1,0:T(8,128)(2,1)} %bitcast.16, bf16[4,5,128,1536]{3,2,1,0:T(8,128)(2,1)} %bitcast.18), custom_call_target="tpu_custom_call" | custom-call | flops 20132659200 | bytes 23592960 | tf_op jit(solution)/shard_map/forward_rows/pallas_call | solution.py:242
  403.6 0.1 reduce-scatter.3.cloned.1.call-update
  403.7 0.1 reduce-scatter.5.cloned.1.call-start
  403.8 51.1 %all-gather.12.cloned.1.call-done = bf16[8192,1536]{1,0:T(8,128)(2,1)} async-done(((bf16[256,1536]{1,0:T(8,128)(2,1)}), bf16[8192,1536]{1,0:T(8,128)(2,1)}) %all-gather.12.cloned.1.call-update) | async-done | bytes 25165840 | tf_op jit(solution)/shard_map/all_gather | solution.py:305
  454.9 39.1 %backward_rows.1 = f32[8,256,1536]{2,1,0:T(8,128)} custom-call(s32[1]{0:T(128)} %bitcast.where, f32[8,4,10,256]{3,2,1,0:T(8,128)} %constant_dynamic-slice_fusion.tab, bf16[8,4,256,1536]{3,2,1,0:T(8,128)(2,1)} %bitcast.14, f32[5,512,1024]{2,1,0:T(8,128)} %get-tuple-element.15.ab_in, bf16[4,5,1536,256]{3,2,1,0:T(8,128)(2,1)} %bitcast.17, ...), custom_call_target="tpu_custom_call" | custom-call | flops 16106127360 | bytes 23592960 | tf_op jit(solution)/shard_map/backward_rows/pallas_call | solution.py:270
  494.0 0.1 reduce-scatter.5.cloned.1.call-update
  494.0 74.5 %weight_grads.1 = (bf16[5,1536,128]{2,1,0:T(8,128)(2,1)}, bf16[5,1536,128]{2,1,0:T(8,128)(2,1)}, bf16[5,128,1536]{2,1,0:T(8,128)(2,1)}) custom-call(f32[8,4,10,256]{3,2,1,0:T(8,128)} %constant_dynamic-slice_fusion.tab, bf16[8,4,256,1536]{3,2,1,0:T(8,128)(2,1)} %bitcast.23, bf16[8,4,256,1536]{3,2,1,0:T(8,128)(2,1)} %bitcast.15, ...), custom_call_target="tpu_custom_call" | custom-call | flops 40265318400 | bytes 50331648 | tf_op jit(solution)/shard_map/weight_grads/pallas_call | solution.py:121
  568.5 0.0 reduce-scatter.3.cloned.1.call-done
  568.5 2.4 convert_bitcast_fusion.1
  570.9 26.6 %reduce-scatter.5.cloned.1.call-done = f32[1,256,1536]{2,1,0:T(8,128)} async-done(((f32[8,256,1536]{2,1,0:T(8,128)}), f32[1,256,1536]{2,1,0:T(8,128)}) %reduce-scatter.5.cloned.1.call-update) | async-done | bytes 1572880 | tf_op jit(solution)/shard_map/reduce_scatter | solution.py:324
  597.4 2.4 convert_bitcast_fusion
  (4 shorter events, 0.1 us)
Async XLA Ops:
  7.2 82.7 %copy-start = (bf16[5,1536,128]{2,1,0:T(8,128)(2,1)S(1)}, bf16[5,1536,128]{2,1,0:T(8,128)(2,1)}, u32[]{:S(2)}) copy-start(bf16[5,1536,128]{2,1,0:T(8,128)(2,1)} %param.10) | copy-start | bytes 5898244
  7.2 82.5 %all-gather.14.cloned.1.call-start = ((), (), s32[]{:S(2)}) async-start(), calls=%async_computation.7 | async-start | bytes 9830400 | tf_op jit(solution)/shard_map/all_gather | solution.py:309
  8.0 124.8 %all-gather.8.cloned.1.call-start = ((), (), s32[]{:S(2)}) async-start(), calls=%async_computation.2 | async-start | bytes 2703360 | tf_op jit(solution)/shard_map/all_gather | solution.py:305
  89.8 186.8 %all-gather.16.cloned.1.call-start = ((), (), s32[]{:S(2)}) async-start(), calls=%async_computation.8 | async-start | bytes 19660800 | tf_op jit(solution)/shard_map/all_gather | solution.py:310
  89.9 2.3 copy-start.1
  93.6 273.2 %all-gather.10.cloned.1.call-start = ((), (), s32[]{:S(2)}) async-start(), calls=%async_computation.3 | async-start | bytes 25952256 | tf_op jit(solution)/shard_map/all_gather | solution.py:305
  94.3 360.6 %all-gather.12.cloned.1.call-start = ((), (), s32[]{:S(2)}) async-start(), calls=%async_computation.5 | async-start | bytes 25952256 | tf_op jit(solution)/shard_map/all_gather | solution.py:305
  94.9 473.6 %reduce-scatter.3.cloned.1.call-start = ((), (), s32[]{:S(2)}) async-start(), calls=%async_computation.4 | async-start | bytes 14155776 | tf_op jit(solution)/shard_map/reduce_scatter | solution.py:322
  403.7 193.7 %reduce-scatter.5.cloned.1.call-start = ((), (), s32[]{:S(2)}) async-start(), calls=%async_computation.6 | async-start | bytes 14155776 | tf_op jit(solution)/shard_map/reduce_scatter | solution.py:324
Sparse Core Ops, SparseCore 0:
  9.6 80.0 all-gather.13
  92.4 40.3 all-gather.7
  134.4 142.1 all-gather.15
  278.5 88.2 all-gather.9
  368.8 86.0 all-gather.11
  457.0 68.4 reduce-scatter.2
  527.8 69.5 reduce-scatter.4

commit v2 on v1

v2 whole, which is shorter than its diff:
```python
import functools

import jax
import jax.numpy as jnp
from jax import lax
from jax.experimental import pallas as pl
from jax.experimental.pallas import tpu as pltpu
from jax.sharding import PartitionSpec as P

BF16 = jnp.bfloat16
F32 = jnp.float32
MESH = pl.DeviceIdType.MESH
VMEM_LIMIT = 62 * 2**20


def slot_count(num_top, tok_dev, experts):
    return 8 * ((5 * num_top * tok_dev + 32 * experts - 1) // (32 * experts))


def dot(a, b):
    return jnp.dot(a, b, preferred_element_type=F32)


def dot_tb(a, b):
    return lax.dot_general(a, b, (((1,), (1,)), ((), ())), preferred_element_type=F32)


def dot_ta(a, b):
    return lax.dot_general(a, b, (((0,), (0,)), ((), ())), preferred_element_type=F32)


def earlier_rows(tok):
    row = lax.broadcasted_iota(jnp.int32, (tok, tok), 0)
    col = lax.broadcasted_iota(jnp.int32, (tok, tok), 1)
    return jnp.where(row < col, 1.0, 0.0).astype(BF16)


def expert_rows(routes, first, own, earlier):
    top = routes.shape[0] // 2
    ids, gates = routes[:top], routes[top:]
    hits = [ids == (first + e).astype(F32) for e in range(own)]
    routed = jnp.concatenate([jnp.sum(jnp.where(m, 1.0, 0.0), axis=0, keepdims=True) for m in hits], axis=0)
    gate = jnp.concatenate([jnp.sum(jnp.where(m, gates, 0.0), axis=0, keepdims=True) for m in hits], axis=0)
    return jnp.where(routed > 0.0, dot(routed.astype(BF16), earlier), -1.0), gate


def hit_masks(pos, cap):
    slot = lax.broadcasted_iota(jnp.int32, (cap, pos.shape[1]), 0).astype(F32)
    return [pos[e : e + 1, :] == slot for e in range(pos.shape[0])]


def one_hot(masks):
    return jnp.concatenate([jnp.where(m, 1.0, 0.0) for m in masks], axis=0).astype(BF16)


def slot_gates(masks, gate):
    return jnp.concatenate([jnp.where(m, gate[e : e + 1, :], 0.0) for e, m in enumerate(masks)], axis=0)


def three_parts(x):
    hi = x.astype(BF16)
    rest = x - hi.astype(F32)
    mid = rest.astype(BF16)
    return hi, mid, (rest - mid.astype(F32)).astype(BF16)


class Links:
    def __init__(self, send_sem, recv_sem):
        self.send_sem, self.recv_sem, self.sent = send_sem, recv_sem, []

    def copy(self, k, src, dst, to):
        return pltpu.make_async_remote_copy(src_ref=src, dst_ref=dst, send_sem=self.send_sem.at[k],
                                            recv_sem=self.recv_sem.at[k], device_id=to, device_id_type=MESH)

    def send(self, src, dst, to):
        k = len(self.sent)
        copy = self.copy(k, src, dst, to)
        copy.start()
        self.sent.append(copy)
        return k

    def arrive(self, k, dst, to):
        self.copy(k, dst, dst, to).wait_recv()

    def drain(self):
        for copy in self.sent:
            copy.wait_send()


def copy_count(own):
    return 9 + 21 * 4 + 7 * own


def gather_kernel(own, cap, width, x_own, dy_own, r_own, w1, w3, w2, x_all, dy_all, r_all, w13_all, w2_all, g1, g3, g2,
                  w13, w2s, xb, dyb, rb, earlier, xs, us, acc13, acc2, send_sem, recv_sem, row_sem, load_sem, w_sem):
    ep, tp = lax.axis_index("ep"), lax.axis_index("tp")
    eps, tps = x_all.shape[0], x_all.shape[1]
    model = x_all.shape[3]
    half = eps // 2
    step = lambda n: lax.rem(ep + (n + eps), eps)
    turn = lambda n: lax.rem(tp + (n + tps), tps)
    right, left, far = step(2), step(-2), step(4)
    mate = ep + 1 - 2 * lax.rem(ep, 2)
    mate_step = lambda n: lax.rem(mate + (n + eps), eps)
    up, down, over = turn(1), turn(-1), turn(2)
    to_right, to_left, to_mate = {"ep": right}, {"ep": left}, {"ep": mate}
    to_up, to_down = {"tp": up}, {"tp": down}
    links = Links(send_sem, recv_sem)

    loads = [pltpu.make_async_copy(w1, w13.at[:, :, pl.ds(0, width)], w_sem.at[0]),
             pltpu.make_async_copy(w3, w13.at[:, :, pl.ds(width, width)], w_sem.at[1]),
             pltpu.make_async_copy(w2, w2s, w_sem.at[2])]
    for copy in loads:
        copy.start()

    barrier = pltpu.get_barrier_semaphore()
    for to in (to_right, to_left, to_mate, to_up, to_down):
        pl.semaphore_signal(barrier, inc=1, device_id=to, device_id_type=MESH)
    pl.semaphore_wait(barrier, 5)

    own_refs, all_refs = (x_own, dy_own, r_own), (x_all, dy_all, r_all)
    upward = (True, False, True)

    def both_ways(kind, src, dst, plus, minus):
        return links.send(src, dst, plus), links.send(src, dst, minus)

    def spread(kinds, t, srcs):
        out = {}
        for kind in kinds:
            dst = all_refs[kind].at[ep, t]
            first, second = (to_right, to_left) if upward[kind] else (to_left, to_right)
            out[kind, upward[kind]] = links.send(srcs[kind], dst, first)
        for kind in kinds:
            dst = all_refs[kind].at[ep, t]
            second = to_left if upward[kind] else to_right
            out[kind, not upward[kind]] = links.send(srcs[kind], dst, second)
        for kind in kinds:
            out[kind, "mate"] = links.send(srcs[kind], all_refs[kind].at[ep, t], to_mate)
        return out

    def pass_on(state, kind, t):
        got, to = (left, to_right) if upward[kind] else (right, to_left)
        block = all_refs[kind].at[got, t]
        links.arrive(state[kind, upward[kind]], block, to)
        state[kind, "far"] = links.send(block, block, to)
        state[kind, "mate1"] = links.send(block, block, to_mate)

    def share(state, kind, t):
        got, to = (right, to_left) if upward[kind] else (left, to_right)
        block = all_refs[kind].at[got, t]
        links.arrive(state[kind, not upward[kind]], block, to)
        state[kind, "mate2"] = links.send(block, block, to_mate)

    def last(state, kind, t):
        block = all_refs[kind].at[far, t]
        links.arrive(state[kind, "far"], block, to_right if upward[kind] else to_left)
        state[kind, "mate3"] = links.send(block, block, to_mate)

    def from_mate(state, t):
        for kind in range(3):
            one, two = (mate_step(-2), mate_step(2)) if upward[kind] else (mate_step(2), mate_step(-2))
            for name, at in (("mate", mate), ("mate1", one), ("mate2", two), ("mate3", mate_step(4))):
                links.arrive(state[kind, name], all_refs[kind].at[at, t], to_mate)

    kinds = (0, 2, 1)

    y_state = {}
    for kind in kinds:
        first = to_up if upward[kind] else to_down
        y_state[kind, upward[kind]] = links.send(own_refs[kind], all_refs[kind].at[ep, tp], first)
    for kind in kinds:
        second = to_down if upward[kind] else to_up
        y_state[kind, not upward[kind]] = links.send(own_refs[kind], all_refs[kind].at[ep, tp], second)
    groups = (tp, down, up, over)
    states = [spread(kinds, tp, own_refs)]
    keep = [pltpu.make_async_copy(own_refs[kind], all_refs[kind].at[ep, tp], row_sem.at[kind]) for kind in range(3)]
    for copy in keep:
        copy.start()
    for copy in loads:
        copy.wait()
    stow = [pltpu.make_async_copy(w13, w13_all.at[tp], w_sem.at[0]), pltpu.make_async_copy(w2s, w2_all.at[tp], w_sem.at[1])]
    for copy in stow:
        copy.start()

    earlier[...] = earlier_rows(earlier.shape[0])
    acc13[...] = jnp.zeros_like(acc13)
    acc2[...] = jnp.zeros_like(acc2)

    cut = 3 * model // 4
    w_state = [None] * own

    def send_weights(e):
        w_state[e] = {(k, s): links.send(ref.at[e], dst.at[tp, e], to)
                      for k, ref, dst in ((0, w13, w13_all), (1, w2s, w2_all)) for s, to in ((True, to_up), (False, to_down))}

    def pass_weights(e):
        state = w_state[e]
        links.arrive(state[0, True], w13_all.at[down, e], to_up)
        head = w13_all.at[down, e, pl.ds(0, cut)]
        state["head"] = links.send(head, head, to_up)
        links.arrive(state[0, False], w13_all.at[up, e], to_down)
        tail = w13_all.at[up, e, pl.ds(cut, model - cut)]
        state["tail"] = links.send(tail, tail, to_down)
        links.arrive(state[1, False], w2_all.at[up, e], to_down)
        state["w2"] = links.send(w2_all.at[up, e], w2_all.at[up, e], to_down)
        links.arrive(state[1, True], w2_all.at[down, e], to_up)

    def have_weights(e):
        state = w_state[e]
        links.arrive(state["head"], w13_all.at[over, e, pl.ds(0, cut)], to_up)
        links.arrive(state["tail"], w13_all.at[over, e, pl.ds(cut, model - cut)], to_down)
        links.arrive(state["w2"], w2_all.at[over, e], to_down)

    def block_loads(t, h):
        at = pl.ds(h * half, half)
        return [pltpu.make_async_copy(src.at[at, t], dst.at[h], load_sem.at[k, h])
                for k, (src, dst) in enumerate(((x_all, xb), (dy_all, dyb), (r_all, rb)))]

    def compute(t):
        for h in range(2):
            for copy in block_loads(t, h):
                copy.start()

        def half_group(h, carry):
            for copy in block_loads(t, h):
                copy.wait()

            def gather(b, carry):
                pos, gate = expert_rows(rb[h, b], ep * own, own, earlier[...])
                masks = hit_masks(pos, cap)
                pick = one_hot(masks)
                gates = jnp.sum(slot_gates(masks, gate), axis=1, keepdims=True)
                rows = pl.ds(pl.multiple_of(b * cap, cap), cap)
                picked = dot(pick, xb[h, b]).astype(BF16)
                for e in range(own):
                    xs[e, rows, :] = picked[e * cap : (e + 1) * cap]
                scaled = (gates * dot(pick, dyb[h, b])).astype(BF16)
                for e in range(own):
                    us[e, rows, :] = scaled[e * cap : (e + 1) * cap]
                return carry

            lax.fori_loop(0, half, gather, 0)

            def expert(e, carry):
                ab = dot(xs[e], w13[e])
                a, b = ab[:, :width], ab[:, width:]
                dh = dot_tb(us[e], w2s[e])
                sig = jax.nn.sigmoid(a)
                silu = a * sig
                h = (silu * b).astype(BF16)
                da = (dh * b * sig * (1.0 + a * (1.0 - sig))).astype(BF16)
                db = (dh * silu).astype(BF16)
                acc13[e] += dot_ta(jnp.concatenate([da, db], axis=1), xs[e])
                acc2[e] += dot_ta(h, us[e])
                return carry

            lax.fori_loop(0, own, expert, 0)
            return carry

        lax.fori_loop(0, 2, half_group, 0)

    def arrivals(g, kinds, what):
        for kind in kinds:
            what(states[g], kind, groups[g])

    def y_arrive(kind, way):
        block = all_refs[kind].at[ep, down if way else up]
        links.arrive(y_state[kind, way], block, to_up if way else to_down)
        return block

    for kind in kinds:
        block = y_arrive(kind, upward[kind])
        y_state[kind, "far"] = links.send(block, block, to_up if upward[kind] else to_down)
    arrivals(0, kinds, pass_on)
    for kind in kinds:
        y_arrive(kind, not upward[kind])
    send_weights(0)
    send_weights(1)
    for g in (1, 2):
        states.append(spread(kinds, groups[g], [ref.at[ep, groups[g]] for ref in all_refs]))
    arrivals(0, kinds, share)
    arrivals(0, kinds, last)
    for kind in kinds:
        links.arrive(y_state[kind, "far"], all_refs[kind].at[ep, over], to_up if upward[kind] else to_down)
    for copy in keep:
        copy.wait()
    from_mate(states[0], groups[0])
    compute(groups[0])

    arrivals(1, kinds, pass_on)
    states.append(spread(kinds, over, [ref.at[ep, over] for ref in all_refs]))
    pass_weights(0)
    send_weights(2)
    arrivals(1, kinds, share)
    arrivals(2, kinds, pass_on)
    pass_weights(1)
    send_weights(3)
    arrivals(2, kinds, share)
    arrivals(1, kinds, last)
    from_mate(states[1], groups[1])
    compute(groups[1])

    arrivals(3, kinds, pass_on)
    pass_weights(2)
    send_weights(4)
    arrivals(3, kinds, share)
    arrivals(2, kinds, last)
    pass_weights(3)
    from_mate(states[2], groups[2])
    compute(groups[2])

    arrivals(3, kinds, last)
    pass_weights(4)
    from_mate(states[3], groups[3])
    compute(groups[3])

    def finish(e, carry):
        g1[e] = acc13[e, :width, :].T.astype(BF16)
        g3[e] = acc13[e, width:, :].T.astype(BF16)
        g2[e] = acc2[e].astype(BF16)
        return carry

    lax.fori_loop(0, own, finish, 0)
    for e in range(own):
        have_weights(e)
    for copy in stow:
        copy.wait()
    links.drain()


def gather_and_wgrad(tokens, d_out, routes, w_one, w_three, w_two, ep_size, tp_size, cap):
    tok, model = tokens.shape
    own, width, _ = w_two.shape
    half = ep_size // 2
    rows = half * cap
    vmem, hbm = pl.BlockSpec(memory_space=pltpu.VMEM), pl.BlockSpec(memory_space=pl.ANY)
    shape = jax.ShapeDtypeStruct
    copies = copy_count(own)
    slot_rows = ep_size * tp_size * cap * own
    return pl.pallas_call(
        functools.partial(gather_kernel, own, cap, width),
        in_specs=[vmem, vmem, vmem, hbm, hbm, hbm],
        out_specs=[hbm] * 5 + [vmem] * 3,
        out_shape=[
            shape((ep_size, tp_size, tok, model), BF16),
            shape((ep_size, tp_size, tok, model), BF16),
            shape((ep_size, tp_size) + routes.shape, F32),
            shape((tp_size, own, model, 2 * width), BF16),
            shape((tp_size, own, width, model), BF16),
            shape((own, model, width), BF16),
            shape((own, model, width), BF16),
            shape((own, width, model), BF16),
        ],
        scratch_shapes=[
            pltpu.VMEM((own, model, 2 * width), BF16),
            pltpu.VMEM((own, width, model), BF16),
            pltpu.VMEM((2, half, tok, model), BF16),
            pltpu.VMEM((2, half, tok, model), BF16),
            pltpu.VMEM((2, half) + routes.shape, F32),
            pltpu.VMEM((tok, tok), BF16),
            pltpu.VMEM((own, rows, model), BF16),
            pltpu.VMEM((own, rows, model), BF16),
            pltpu.VMEM((own, 2 * width, model), F32),
            pltpu.VMEM((own, width, model), F32),
            pltpu.SemaphoreType.DMA((copies,)),
            pltpu.SemaphoreType.DMA((copies,)),
            pltpu.SemaphoreType.DMA((3,)),
            pltpu.SemaphoreType.DMA((3, 2)),
            pltpu.SemaphoreType.DMA((3,)),
        ],
        compiler_params=pltpu.CompilerParams(vmem_limit_bytes=VMEM_LIMIT, collective_id=0, has_side_effects=True),
        cost_estimate=pl.CostEstimate(
            flops=2 * slot_rows * model * (2 * tok + 6 * width),
            bytes_accessed=4 * ep_size * tp_size * tok * model,
            transcendentals=0,
        ),
        name="gather_and_wgrad",
    )(tokens, d_out, routes, w_one, w_three, w_two)


def forward_kernel(own, cap, width, where, routes, x, w13, w2, y_out, ab_out, earlier, xs, ys):
    step = pl.program_id(0)
    blocks, shards = ys.shape[0], w13.shape[0]
    first = where[1] * own

    @pl.when(step == 0)
    def _():
        earlier[...] = earlier_rows(earlier.shape[0])

    @pl.when(step < blocks)
    def _():
        pos, _ = expert_rows(routes[step, 0], first, own, earlier[...])
        picked = dot(one_hot(hit_masks(pos, cap)), x[0, 0]).astype(BF16)
        rows = pl.ds(pl.multiple_of(step * cap, cap), cap)
        for e in range(own):
            xs[e, rows, :] = picked[e * cap : (e + 1) * cap]

    @pl.when((step >= blocks) & (step < blocks + own))
    def _():
        e = step - blocks
        parts = []
        for j in range(shards):
            ab = dot(xs[e], w13[j, 0])
            ab_out[0, :, 2 * width * j : 2 * width * (j + 1)] = ab
            a, b = ab[:, :width], ab[:, width:]
            parts.append((a * jax.nn.sigmoid(a) * b).astype(BF16))
        h = jnp.concatenate(parts, axis=1)
        y = dot(h, w2[:, 0].reshape(shards * width, w2.shape[3])).astype(BF16)
        at = pl.ds(pl.multiple_of(e * cap, cap), cap)
        for k in range(blocks):
            ys[k, at, :] = y[k * cap : (k + 1) * cap]

    @pl.when(step >= blocks + own)
    def _():
        k = step - blocks - own
        pos, gate = expert_rows(routes[k, 0], first, own, earlier[...])
        hi, mid, low = three_parts(slot_gates(hit_masks(pos, cap), gate))
        rows = ys[k]
        y_out[0] = dot_ta(hi, rows) + (dot_ta(mid, rows) + dot_ta(low, rows))


def backward_kernel(own, cap, width, where, routes, dy, ab_in, w13, w2, dx_out, earlier, us, vs):
    step = pl.program_id(0)
    blocks, shards = vs.shape[0], w13.shape[0]
    first = where[1] * own

    @pl.when(step == 0)
    def _():
        earlier[...] = earlier_rows(earlier.shape[0])

    @pl.when(step < blocks)
    def _():
        pos, gate = expert_rows(routes[step, 0], first, own, earlier[...])
        masks = hit_masks(pos, cap)
        gates = jnp.sum(slot_gates(masks, gate), axis=1, keepdims=True)
        scaled = (gates * dot(one_hot(masks), dy[0, 0])).astype(BF16)
        rows = pl.ds(pl.multiple_of(step * cap, cap), cap)
        for e in range(own):
            us[e, rows, :] = scaled[e * cap : (e + 1) * cap]

    @pl.when((step >= blocks) & (step < blocks + own))
    def _():
        e = step - blocks
        v = None
        for j in range(shards):
            dh = dot_tb(us[e], w2[j, 0])
            a = ab_in[0, :, 2 * width * j : 2 * width * j + width]
            b = ab_in[0, :, 2 * width * j + width : 2 * width * (j + 1)]
            sig = jax.nn.sigmoid(a)
            da = (dh * b * sig * (1.0 + a * (1.0 - sig))).astype(BF16)
            db = (dh * (a * sig)).astype(BF16)
            part = dot_tb(jnp.concatenate([da, db], axis=1), w13[j, 0])
            v = part if v is None else v + part
        v = v.astype(BF16)
        at = pl.ds(pl.multiple_of(e * cap, cap), cap)
        for k in range(blocks):
            vs[k, at, :] = v[k * cap : (k + 1) * cap]

    @pl.when(step >= blocks + own)
    def _():
        k = step - blocks - own
        pos, _ = expert_rows(routes[k, 0], first, own, earlier[...])
        dx_out[0] = dot_ta(one_hot(hit_masks(pos, cap)), vs[k])


def token_specs(blocks, own, tok, model, width, shards, routes):
    expert = lambda s: jnp.clip(s - blocks, 0, own - 1)
    return dict(
        routes=pl.BlockSpec((blocks, 1, routes, tok), lambda s, w: (0, w[0], 0, 0)),
        rows=pl.BlockSpec((1, 1, tok, model), lambda s, w: (jnp.minimum(s, blocks - 1), w[0], 0, 0)),
        w13=pl.BlockSpec((shards, 1, model, 2 * width), lambda s, w: (0, expert(s), 0, 0)),
        w2=pl.BlockSpec((shards, 1, width, model), lambda s, w: (0, expert(s), 0, 0)),
        out=pl.BlockSpec((1, tok, model), lambda s, w: (jnp.clip(s - blocks - own, 0, blocks - 1), 0, 0)),
        act=lambda rows: pl.BlockSpec((1, rows, 2 * width * shards), lambda s, w: (expert(s), 0, 0)),
    )


def forward_rows(where, routes, x_all, w13_all, w2_all, cap):
    blocks, _, tok, model = x_all.shape
    shards, own, width, _ = w2_all.shape
    rows = blocks * cap
    specs = token_specs(blocks, own, tok, model, width, shards, routes.shape[2])
    return pl.pallas_call(
        functools.partial(forward_kernel, own, cap, width),
        grid_spec=pltpu.PrefetchScalarGridSpec(
            num_scalar_prefetch=1,
            grid=(2 * blocks + own,),
            in_specs=[specs["routes"], specs["rows"], specs["w13"], specs["w2"]],
            out_specs=[specs["out"], specs["act"](rows)],
            scratch_shapes=[pltpu.VMEM((tok, tok), BF16), pltpu.VMEM((own, rows, model), BF16),
                            pltpu.VMEM((blocks, own * cap, model), BF16)],
        ),
        out_shape=[
            jax.ShapeDtypeStruct((blocks, tok, model), F32),
            jax.ShapeDtypeStruct((own, rows, 2 * width * shards), F32),
        ],
        compiler_params=pltpu.CompilerParams(vmem_limit_bytes=VMEM_LIMIT),
        cost_estimate=pl.CostEstimate(
            flops=2 * own * rows * model * (4 * tok + 3 * width * shards),
            bytes_accessed=2 * own * 3 * model * width * shards,
            transcendentals=0,
        ),
        name="forward_rows",
    )(where, routes, x_all, w13_all, w2_all)


def backward_rows(where, routes, dy_all, ab, w13_all, w2_all, cap):
    blocks, _, tok, model = dy_all.shape
    shards, own, width, _ = w2_all.shape
    rows = blocks * cap
    specs = token_specs(blocks, own, tok, model, width, shards, routes.shape[2])
    return pl.pallas_call(
        functools.partial(backward_kernel, own, cap, width),
        grid_spec=pltpu.PrefetchScalarGridSpec(
            num_scalar_prefetch=1,
            grid=(2 * blocks + own,),
            in_specs=[specs["routes"], specs["rows"], specs["act"](rows), specs["w13"], specs["w2"]],
            out_specs=specs["out"],
            scratch_shapes=[pltpu.VMEM((tok, tok), BF16), pltpu.VMEM((own, rows, model), BF16),
                            pltpu.VMEM((blocks, own * cap, model), BF16)],
        ),
        out_shape=jax.ShapeDtypeStruct((blocks, tok, model), F32),
        compiler_params=pltpu.CompilerParams(vmem_limit_bytes=VMEM_LIMIT),
        cost_estimate=pl.CostEstimate(
            flops=2 * own * rows * model * (2 * tok + 3 * width * shards),
            bytes_accessed=2 * own * 3 * model * width * shards,
            transcendentals=0,
        ),
        name="backward_rows",
    )(where, routes, dy_all, ab, w13_all, w2_all)


def solution(mesh):
    ep_size, tp_size = mesh.shape["ep"], mesh.shape["tp"]
    row_spec = P(("dp", "ep", "tp"), None)
    col_spec = P("ep", None, "tp")
    down_spec = P("ep", "tp", None)
    grad_col = P(("dp", "ep"), None, "tp")
    grad_down = P(("dp", "ep"), "tp", None)

    def local_step(tokens, expert_ids, gate_vals, w_one, w_three, w_two, d_out):
        cap = slot_count(expert_ids.shape[1], tokens.shape[0], w_one.shape[0] * ep_size)
        routes = jnp.concatenate([expert_ids.T.astype(F32), gate_vals.T], axis=0)
        where = jnp.stack([lax.axis_index("tp"), lax.axis_index("ep")]).astype(jnp.int32)

        x_all, dy_all, r_all, w13_all, w2_all, grad_one, grad_three, grad_two = gather_and_wgrad(
            tokens, d_out, routes, w_one, w_three, w_two, ep_size, tp_size, cap)
        y_part, ab = forward_rows(where, r_all, x_all, w13_all, w2_all, cap)
        out = lax.psum_scatter(y_part, "ep", scatter_dimension=0, tiled=False).astype(BF16)
        dx_part = backward_rows(where, r_all, dy_all, ab, w13_all, w2_all, cap)
        dx = lax.psum_scatter(dx_part, "ep", scatter_dimension=0, tiled=False).astype(BF16)
        return out, dx, grad_one, grad_three, grad_two

    return jax.shard_map(local_step, mesh=mesh,
                         in_specs=(row_spec, row_spec, row_spec, col_spec, col_spec, down_spec, row_spec),
                         out_specs=(row_spec, row_spec, grad_col, grad_col, grad_down), check_vma=False)
```

time: 607 us -> 461 us (0.76)
  waiting for transfers between devices: 429 us -> 96.4 us
  Pallas kernels: 150 us -> 337 us
    all_gather x5 -> x0, waiting for transfers between devices: 400 us -> none  [the longest x3 179 us: everyone(): full = lax.all_gather(rows, ('ep', 'tp'), axis=0, tiled=True)]
    pallas_call x1, Pallas kernels: 74.5 us -> 256 us  [gather_and_wgrad(): pl.pallas_call(functools.partial(gather_kernel, own, cap, width), in_spec...]
    reduce_scatter x1, waiting for transfers between devices: 26.6 us -> 69.5 us  [local_step(): lax.psum_scatter(dx_part, 'ep', scatter_dimension=0, tiled=False)]
    reduce_scatter x1, waiting for transfers between devices: 0.01 us -> 26.8 us  [local_step(): lax.psum_scatter(y_part, 'ep', scatter_dimension=0, tiled=False)]
  transfers between devices with their start and end apart: 7 -> 2, of which waited for: 6 -> 2; matrix products, arithmetic and copies ran while one was open for 2% -> 1% of each run, Pallas kernels for 25% -> 9%
where the time goes in v2:
time: 461 us
  Pallas kernels  337 us (73%)
  waiting for transfers between devices  96.4 us (21%)
  between operations  14.1 us (3%)
  other arithmetic  7.32 us (2%)
  local copies, waits for them, and re-layouts  5.78 us (1%)
    pallas_call x1, Pallas kernels, gather_and_wgrad(): pl.pallas_call(functools.partial(gather_kernel, own, cap, width), in_spec...  256 us
    reduce_scatter x1, waiting for transfers between devices, local_step(): lax.psum_scatter(dx_part, 'ep', scatter_dimension=0, tiled=False)  69.5 us
    pallas_call x1, Pallas kernels, backward_rows(): pl.pallas_call(functools.partial(backward_kernel, own, cap, width), grid_...  41.6 us
    pallas_call x1, Pallas kernels, forward_rows(): pl.pallas_call(functools.partial(forward_kernel, own, cap, width), grid_s...  39.6 us
    reduce_scatter x1, waiting for transfers between devices, local_step(): lax.psum_scatter(y_part, 'ep', scatter_dimension=0, tiled=False)  26.8 us
  transfers between devices with their start and end apart: 2, of which 2 were waited for; matrix products, arithmetic and copies ran while one was open for 1% of the time, Pallas kernels for 9%

profile of v2, /device:TPU:97, one launch (start us, length us, event | category | flops | bytes accessed | tf_op | source)
XLA Modules:
  0.0 460.7 jit_solution(4874495865588197421)
XLA Ops:
  7.2 0.1 reduce-scatter.3.cloned.1.call-start
  7.3 0.7 convert_bitcast_fusion.2
  8.0 0.6 pad_add_fusion.where
  8.5 1.3 pad_maximum_fusion.r_own
  9.8 255.7 %gather_and_wgrad.1 = (bf16[8,4,256,1536]{3,2,1,0:T(8,128)(2,1)}, bf16[8,4,256,1536]{3,2,1,0:T(8,128)(2,1)}, f32[8,4,16,256]{3,2,1,0:T(8,128)}, bf16[4,5,1536,25...) custom-call(bf16[256,1536]{1,0:T(8,128)(2,1)} %x_own.1, ...), custom_call_target="tpu_custom_call" | custom-call | flops 40265318400 | bytes 50331648 | tf_op jit(solution)/shard_map/gather_and_wgrad/pallas_call | solution.py:340
  265.6 39.6 %forward_rows.1 = (f32[8,256,1536]{2,1,0:T(8,128)}, f32[5,512,1024]{2,1,0:T(8,128)}) custom-call(s32[2]{0:T(128)} %pad_add_fusion.where, f32[8,4,16,256]{3,2,1,0:T(8,128)} %get-tuple-element.15.routes, bf16[8,4,256,1536]{3,2,1,0:T(8,128)(2,1)} %get-tuple-element.16.x, bf16[4,5,1536,256]{3,2,1,0:T(8,128)(2,1)} %get-tuple-element.17.w13, ...), custom_call_target="tpu_custom_call" | custom-call | flops 20132659200 | bytes 23592960 | tf_op jit(solution)/shard_map/forward_rows/pallas_call | solution.py:483
  305.2 0.1 reduce-scatter.3.cloned.1.call-update
  305.3 0.1 reduce-scatter.5.cloned.1.call-start
  305.4 41.6 %backward_rows.1 = f32[8,256,1536]{2,1,0:T(8,128)} custom-call(s32[2]{0:T(128)} %pad_add_fusion.where, f32[8,4,16,256]{3,2,1,0:T(8,128)} %get-tuple-element.15.routes, bf16[8,4,256,1536]{3,2,1,0:T(8,128)(2,1)} %get-tuple-element.20.dy, f32[5,512,1024]{2,1,0:T(8,128)} %get-tuple-element.21.ab_in, bf16[4,5,1536,256]{3,2,1,0:T(8,128)(2,1)} %get-tuple-element.17.w13, ...), custom_call_target="tpu_custom_call" | custom-call | flops 16106127360 | bytes 23592960 | tf_op jit(solution)/shard_map/backward_rows/pallas_call | solution.py:512
  347.0 0.1 reduce-scatter.5.cloned.1.call-update
  347.0 0.0 copy-start.2
  347.0 26.8 %reduce-scatter.3.cloned.1.call-done = f32[1,256,1536]{2,1,0:T(8,128)} async-done(((f32[8,256,1536]{2,1,0:T(8,128)}), f32[1,256,1536]{2,1,0:T(8,128)}) %reduce-scatter.3.cloned.1.call-update) | async-done | bytes 1572880 | tf_op jit(solution)/shard_map/reduce_scatter | solution.py:549
  373.9 2.4 convert_bitcast_fusion.1
  376.2 69.5 %reduce-scatter.5.cloned.1.call-done = f32[1,256,1536]{2,1,0:T(8,128)} async-done(((f32[8,256,1536]{2,1,0:T(8,128)}), f32[1,256,1536]{2,1,0:T(8,128)}) %reduce-scatter.5.cloned.1.call-update) | async-done | bytes 1572880 | tf_op jit(solution)/shard_map/reduce_scatter | solution.py:551
  445.7 2.4 convert_bitcast_fusion
  448.1 0.0 copy-done.2
  448.1 0.0 copy-start.1
  448.1 1.3 copy.15
  449.4 1.0 copy-done.1
  450.3 0.0 copy-start
  450.3 1.3 copy.16
  451.6 1.0 copy-done
  452.6 1.3 copy.17
Async XLA Ops:
  7.2 366.7 %reduce-scatter.3.cloned.1.call-start = ((), (), s32[]{:S(2)}) async-start(), calls=%async_computation.2 | async-start | bytes 14155776 | tf_op jit(solution)/shard_map/reduce_scatter | solution.py:549
  305.3 140.4 %reduce-scatter.5.cloned.1.call-start = ((), (), s32[]{:S(2)}) async-start(), calls=%async_computation.3 | async-start | bytes 14155776 | tf_op jit(solution)/shard_map/reduce_scatter | solution.py:551
  347.0 101.0 %copy-start.2 = (bf16[5,1536,128]{2,1,0:T(8,128)(2,1)S(1)}, bf16[5,1536,128]{2,1,0:T(8,128)(2,1)}, u32[]{:S(2)}) copy-start(bf16[5,1536,128]{2,1,0:T(8,128)(2,1)} %get-tuple-element.32) | copy-start | bytes 5898244
  448.1 2.3 copy-start.1
  450.3 2.3 copy-start
Sparse Core Ops, SparseCore 0:
  305.4 68.4 reduce-scatter.2
  376.2 69.4 reduce-scatter.4

commit v3 on v0

v3 whole, which is shorter than its diff:
```python
import functools

import jax
import jax.numpy as jnp
from jax import lax
from jax.experimental import pallas as pl
from jax.experimental.pallas import tpu as pltpu
from jax.sharding import PartitionSpec as P

BF16 = jnp.bfloat16
F32 = jnp.float32
MESH = pl.DeviceIdType.MESH
VMEM_LIMIT = 62 * 2**20


def slot_count(num_top, tok_dev, experts):
    return 8 * ((5 * num_top * tok_dev + 32 * experts - 1) // (32 * experts))


def dot(a, b):
    return jnp.dot(a, b, preferred_element_type=F32)


def dot_tb(a, b):
    return lax.dot_general(a, b, (((1,), (1,)), ((), ())), preferred_element_type=F32)


def dot_ta(a, b):
    return lax.dot_general(a, b, (((0,), (0,)), ((), ())), preferred_element_type=F32)


def earlier_rows(tok):
    row = lax.broadcasted_iota(jnp.int32, (tok, tok), 0)
    col = lax.broadcasted_iota(jnp.int32, (tok, tok), 1)
    return jnp.where(row < col, 1.0, 0.0).astype(BF16)


def expert_rows(routes, first, own, earlier):
    top = routes.shape[0] // 2
    ids, gates = routes[:top], routes[top:]
    hits = [ids == (first + e).astype(F32) for e in range(own)]
    routed = jnp.concatenate([jnp.sum(jnp.where(m, 1.0, 0.0), axis=0, keepdims=True) for m in hits], axis=0)
    gate = jnp.concatenate([jnp.sum(jnp.where(m, gates, 0.0), axis=0, keepdims=True) for m in hits], axis=0)
    return jnp.where(routed > 0.0, dot(routed.astype(BF16), earlier), -1.0), gate


def hit_masks(pos, cap):
    slot = lax.broadcasted_iota(jnp.int32, (cap, pos.shape[1]), 0).astype(F32)
    return [pos[e : e + 1, :] == slot for e in range(pos.shape[0])]


def one_hot(masks):
    return jnp.concatenate([jnp.where(m, 1.0, 0.0) for m in masks], axis=0).astype(BF16)


def slot_gates(masks, gate):
    return jnp.concatenate([jnp.where(m, gate[e : e + 1, :], 0.0) for e, m in enumerate(masks)], axis=0)


def three_parts(x):
    hi = x.astype(BF16)
    rest = x - hi.astype(F32)
    mid = rest.astype(BF16)
    return hi, mid, (rest - mid.astype(F32)).astype(BF16)


class Links:
    def __init__(self, send_sem, recv_sem):
        self.send_sem, self.recv_sem, self.sent, self.finished = send_sem, recv_sem, [], set()

    def copy(self, k, src, dst, to):
        return pltpu.make_async_remote_copy(src_ref=src, dst_ref=dst, send_sem=self.send_sem.at[k],
                                            recv_sem=self.recv_sem.at[k], device_id=to, device_id_type=MESH)

    def send(self, src, dst, to):
        k = len(self.sent)
        copy = self.copy(k, src, dst, to)
        copy.start()
        self.sent.append(copy)
        return k

    def arrive(self, k, dst, to):
        self.copy(k, dst, dst, to).wait_recv()

    def finish(self, k):
        self.finished.add(k)
        self.sent[k].wait_send()

    def drain(self):
        for k in range(len(self.sent)):
            if k not in self.finished:
                self.finish(k)


def copy_count(own):
    return 9 + 21 * 4 + 7 * own + 2 * 10


def layer_kernel(own, cap, width, x_own, dy_own, r_own, w1, w3, w2, x_all, dy_all, r_all, w13_all, w2_all, xs_all, us_all,
                 ys_all, sums, mate_land, half_land, last_land, g1, g3, g2, w13, w2s, xb, dyb, rb, routes, earlier, xs, us,
                 acc13, acc2, g_buf, w13e, w2e, ab_buf, h_buf, d_buf, y_buf, v_buf, c_buf, gates_buf, give, keep_sum, mate_sum,
                 turn_sum, send_sem, recv_sem, row_sem, load_sem, w_sem, slot_sem, in_sem, out_sem, c_sem, sum_sem, g_sem):
    ep, tp = lax.axis_index("ep"), lax.axis_index("tp")
    eps, tps = x_all.shape[0], x_all.shape[1]
    model = x_all.shape[3]
    side = model // 2
    half = eps // 2
    step = lambda n: lax.rem(ep + (n + eps), eps)
    turn = lambda n: lax.rem(tp + (n + tps), tps)
    right, left, far = step(2), step(-2), step(4)
    mate = ep + 1 - 2 * lax.rem(ep, 2)
    mate_step = lambda n: lax.rem(mate + (n + eps), eps)
    up, down, over = turn(1), turn(-1), turn(2)
    to_right, to_left, to_mate = {"ep": right}, {"ep": left}, {"ep": mate}
    to_up, to_down = {"tp": up}, {"tp": down}
    links = Links(send_sem, recv_sem)
    wide = 512 if model % 512 == 0 else model

    loads = [pltpu.make_async_copy(w1, w13.at[:, :, pl.ds(0, width)], w_sem.at[0]),
             pltpu.make_async_copy(w3, w13.at[:, :, pl.ds(width, width)], w_sem.at[1]),
             pltpu.make_async_copy(w2, w2s, w_sem.at[2])]
    for copy in loads:
        copy.start()

    barrier = pltpu.get_barrier_semaphore()
    for to in (to_right, to_left, to_mate, to_up, to_down):
        pl.semaphore_signal(barrier, inc=1, device_id=to, device_id_type=MESH)
    pl.semaphore_wait(barrier, 5)

    own_refs, all_refs = (x_own, dy_own, r_own), (x_all, dy_all, r_all)
    upward = (True, False, True)
    kinds = (0, 2, 1)

    def spread(t, srcs):
        out = {}
        for kind in kinds:
            to = to_right if upward[kind] else to_left
            out[kind, upward[kind]] = links.send(srcs[kind], all_refs[kind].at[ep, t], to)
        for kind in kinds:
            to = to_left if upward[kind] else to_right
            out[kind, not upward[kind]] = links.send(srcs[kind], all_refs[kind].at[ep, t], to)
        for kind in kinds:
            out[kind, "mate"] = links.send(srcs[kind], all_refs[kind].at[ep, t], to_mate)
        return out

    def pass_on(g):
        state, t = states[g], groups[g]
        for kind in kinds:
            got, to = (left, to_right) if upward[kind] else (right, to_left)
            block = all_refs[kind].at[got, t]
            links.arrive(state[kind, upward[kind]], block, to)
            state[kind, "far"] = links.send(block, block, to)
            state[kind, "mate1"] = links.send(block, block, to_mate)

    def share(g):
        state, t = states[g], groups[g]
        for kind in kinds:
            got, to = (right, to_left) if upward[kind] else (left, to_right)
            block = all_refs[kind].at[got, t]
            links.arrive(state[kind, not upward[kind]], block, to)
            state[kind, "mate2"] = links.send(block, block, to_mate)

    def last(g):
        state, t = states[g], groups[g]
        for kind in kinds:
            block = all_refs[kind].at[far, t]
            links.arrive(state[kind, "far"], block, to_right if upward[kind] else to_left)
            state[kind, "mate3"] = links.send(block, block, to_mate)

    def from_mate(g):
        state, t = states[g], groups[g]
        for kind in kinds:
            one, two = (mate_step(-2), mate_step(2)) if upward[kind] else (mate_step(2), mate_step(-2))
            for name, at in (("mate", mate), ("mate1", one), ("mate2", two), ("mate3", mate_step(4))):
                links.arrive(state[kind, name], all_refs[kind].at[at, t], to_mate)

    cut = 3 * model // 4
    w_state = [None] * own

    def send_weights(e):
        w_state[e] = {(k, s): links.send(ref.at[e], dst.at[tp, e], to)
                      for k, ref, dst in ((0, w13, w13_all), (1, w2s, w2_all)) for s, to in ((True, to_up), (False, to_down))}

    def pass_weights(e):
        state = w_state[e]
        links.arrive(state[0, True], w13_all.at[down, e], to_up)
        head = w13_all.at[down, e, pl.ds(0, cut)]
        state["head"] = links.send(head, head, to_up)
        links.arrive(state[0, False], w13_all.at[up, e], to_down)
        tail = w13_all.at[up, e, pl.ds(cut, model - cut)]
        state["tail"] = links.send(tail, tail, to_down)
        links.arrive(state[1, False], w2_all.at[up, e], to_down)
        state["w2"] = links.send(w2_all.at[up, e], w2_all.at[up, e], to_down)
        links.arrive(state[1, True], w2_all.at[down, e], to_up)

    def have_weights(e):
        state = w_state[e]
        links.arrive(state["head"], w13_all.at[over, e, pl.ds(0, cut)], to_up)
        links.arrive(state["tail"], w13_all.at[over, e, pl.ds(cut, model - cut)], to_down)
        links.arrive(state["w2"], w2_all.at[over, e], to_down)

    def pair_loads(t, h, p):
        at = pl.ds(h * half + p * (half // 2), half // 2)
        return [pltpu.make_async_copy(src.at[at, t], dst.at[p], load_sem.at[k, p])
                for k, (src, dst) in enumerate(((x_all, xb), (dy_all, dyb), (r_all, rb)))]

    def compute(t, keep):
        for p in range(2):
            for copy in pair_loads(t, 0, p):
                copy.start()

        def half_group(h, carry):
            for p in range(2):
                for copy in pair_loads(t, h, p):
                    copy.wait()

                def gather(b, carry):
                    pos, gate = expert_rows(rb[p, b], ep * own, own, earlier[...])
                    masks = hit_masks(pos, cap)
                    pick = one_hot(masks)
                    gates = jnp.sum(slot_gates(masks, gate), axis=1, keepdims=True)
                    rows = pl.ds(pl.multiple_of((p * (half // 2) + b) * cap, cap), cap)
                    picked = dot(pick, xb[p, b]).astype(BF16)
                    for e in range(own):
                        xs[e, rows, :] = picked[e * cap : (e + 1) * cap]
                    scaled = (gates * dot(pick, dyb[p, b])).astype(BF16)
                    for e in range(own):
                        us[e, rows, :] = scaled[e * cap : (e + 1) * cap]
                    return carry

                lax.fori_loop(0, half // 2, gather, 0)

                @pl.when(h == 0)
                def _():
                    for copy in pair_loads(t, 1, p):
                        copy.start()

            stores = []
            if keep:
                stores = [pltpu.make_async_copy(xs, xs_all.at[:, h], slot_sem.at[0]),
                          pltpu.make_async_copy(us, us_all.at[:, h], slot_sem.at[1])]
            for copy in stores:
                copy.start()

            def expert(e, carry):
                ab = dot(xs[e], w13[e])
                a, b = ab[:, :width], ab[:, width:]
                dh = dot_tb(us[e], w2s[e])
                sig = jax.nn.sigmoid(a)
                silu = a * sig
                hid = (silu * b).astype(BF16)
                da = (dh * b * sig * (1.0 + a * (1.0 - sig))).astype(BF16)
                db = (dh * silu).astype(BF16)
                acc13[e] += dot_ta(jnp.concatenate([da, db], axis=1), xs[e])
                acc2[e] += dot_ta(hid, us[e])
                return carry

            lax.fori_loop(0, own, expert, 0)
            for copy in stores:
                copy.wait()
            return carry

        lax.fori_loop(0, 2, half_group, 0)

    def fetch(e):
        copies = [pltpu.make_async_copy(xs_all.at[e], xs.at[pl.ds(0, 2)], in_sem.at[0]),
                  pltpu.make_async_copy(us_all.at[e], us.at[pl.ds(0, 2)], in_sem.at[1]),
                  pltpu.make_async_copy(w2_all.at[:, e], w2e, in_sem.at[2])]
        copies += [pltpu.make_async_copy(w13_all.at[j, e], w13e.at[j], in_sem.at[3 + j]) for j in range(tps)]
        for k in (0, 3, 4, 5, 6, 2, 1):
            copies[k].start()
        return copies

    slots = eps * cap
    pending = {}

    def put(name, buf, e, value, at):
        for k in range(eps):
            buf[k, :, at] = value[k * cap : (k + 1) * cap]

    def store_rows(kind, buf, e):
        copy = pltpu.make_async_copy(buf, ys_all.at[kind, :, e], out_sem.at[kind])
        copy.start()
        pending[kind] = copy

    def settle_rows(kind):
        if kind in pending:
            pending.pop(kind).wait()

    def forward(e, copies):
        copies[0].wait()

        def shard(j, carry):
            pltpu.make_async_copy(w13_all.at[j, e], w13e.at[j], in_sem.at[3 + j]).wait()
            ab = dot(xs[0:2].reshape(slots, model), w13e[j])
            ab_buf[j] = ab
            a, b = ab[:, :width], ab[:, width:]
            h_buf[:, pl.ds(pl.multiple_of(j * width, width), width)] = (a * jax.nn.sigmoid(a) * b).astype(BF16)
            return carry

        lax.fori_loop(0, tps, shard, 0)
        copies[2].wait()
        settle_rows(0)

        def columns(n, carry):
            at = pl.ds(pl.multiple_of(n * wide, wide), wide)
            put("y", y_buf, e, dot(h_buf[...], w2e[:, :, at].reshape(tps * width, wide)).astype(BF16), at)
            return carry

        lax.fori_loop(0, model // wide, columns, 0)
        store_rows(0, y_buf, e)

    def backward(e, copies):
        copies[1].wait()

        def shard(j, carry):
            dh = dot_tb(us[0:2].reshape(slots, model), w2e[j])
            a, b = ab_buf[j, :, :width], ab_buf[j, :, width:]
            sig = jax.nn.sigmoid(a)
            d_buf[j, :, :width] = (dh * b * sig * (1.0 + a * (1.0 - sig))).astype(BF16)
            d_buf[j, :, width:] = (dh * (a * sig)).astype(BF16)
            return carry

        lax.fori_loop(0, tps, shard, 0)
        settle_rows(1)

        def columns(n, carry):
            at = pl.ds(pl.multiple_of(n * wide, wide), wide)
            v = dot_tb(d_buf[0], w13e[0, at, :])
            for j in range(1, tps):
                v = v + dot_tb(d_buf[j], w13e[j, at, :])
            put("v", v_buf, e, v.astype(BF16), at)
            return carry

        lax.fori_loop(0, model // wide, columns, 0)
        store_rows(1, v_buf, e)

    def expert(e):
        have_weights(e)
        copies = fetch(e)
        forward(e, copies)
        backward(e, copies)

    offsets = (4, 2, -2, 0)

    def row_load(kind, block, slot):
        return pltpu.make_async_copy(ys_all.at[kind, block], c_buf.at[slot], c_sem.at[slot])

    def combine(kind, block, slot, tile):
        pos, gate = expert_rows(routes[block], ep * own, own, earlier[...])
        masks = hit_masks(pos, cap)
        parts = three_parts(slot_gates(masks, gate)) if kind == 0 else (one_hot(masks),)
        for k, part in enumerate(parts):
            gates_buf[k] = part
        row_load(kind, block, slot).wait()
        for s in range(2):
            total = None
            rows = c_buf[slot, :, :, s * side : (s + 1) * side].reshape(own * cap, side)
            for k in reversed(range(len(parts))):
                term = dot_ta(gates_buf[k], rows)
                total = term if total is None else total + term
            tile[s] = total

    def sum_up(kind):
        settle_rows(kind)
        state = {}
        blocks = [(mate_step(o), step(o)) for o in offsets]
        order = [b for pair in blocks for b in pair]
        row_load(kind, order[0], 0).start()

        def one(n, tile):
            if n + 1 < len(order):
                row_load(kind, order[n + 1], (n + 1) % 2).start()
            combine(kind, order[n], n % 2, tile)

        gifts, writes = [], []

        def give_block(i):
            if i >= 2:
                links.finish(gifts[i - 2])
            one(2 * i, give.at[i % 2])
            gifts.append(links.send(give.at[i % 2], mate_land.at[kind, i], to_mate))

        def own_block(i):
            one(2 * i + 1, keep_sum.at[i % 2])

        def add_mate(i):
            links.arrive(gifts[i], mate_land.at[kind, i], to_mate)
            copy = pltpu.make_async_copy(mate_land.at[kind, i], mate_sum, sum_sem.at[0])
            copy.start()
            copy.wait()
            keep_sum[i % 2] += mate_sum[...]
            writes.append(pltpu.make_async_copy(keep_sum.at[i % 2], sums.at[kind, i], sum_sem.at[1 + i % 2]))
            writes[i].start()

        def send_sum(i):
            writes[i].wait()
            if i == 0:
                state["far right"] = links.send(sums.at[kind, 0, 0], half_land.at[kind, 0], to_right)
                state["far left"] = links.send(sums.at[kind, 0, 1], half_land.at[kind, 1], to_left)
            elif i == 1:
                state["right"] = links.send(sums.at[kind, 1, 1], last_land.at[kind, 0, 1], to_right)
            elif i == 2:
                state["left"] = links.send(sums.at[kind, 2, 0], last_land.at[kind, 1, 0], to_left)

        give_block(0)
        own_block(0)
        give_block(1)
        add_mate(0)
        send_sum(0)
        own_block(1)
        give_block(2)
        add_mate(1)
        own_block(2)
        send_sum(1)
        give_block(3)
        add_mate(2)
        own_block(3)
        send_sum(2)
        add_mate(3)
        send_sum(3)
        links.finish(gifts[2])
        links.finish(gifts[3])
        return state

    def turn_sums(kind, state):
        for s, key, to, back in ((0, "far right", to_right, to_right), (1, "far left", to_left, to_left)):
            links.arrive(state[key], half_land.at[kind, s], back)
            tile = turn_sum.at[kind, s]
            a = pltpu.make_async_copy(sums.at[kind, 1 + s, s], tile, sum_sem.at[0])
            b = pltpu.make_async_copy(half_land.at[kind, s], mate_sum.at[s], sum_sem.at[1])
            a.start()
            b.start()
            a.wait()
            b.wait()
            turn_sum[kind, s] += mate_sum[s]
            state["turn", s] = links.send(tile, last_land.at[kind, s, s], to)

    def sums_here(kind, state):
        links.arrive(state["right"], last_land.at[kind, 0, 1], to_right)
        links.arrive(state["left"], last_land.at[kind, 1, 0], to_left)
        links.arrive(state["turn", 0], last_land.at[kind, 0, 0], to_right)
        links.arrive(state["turn", 1], last_land.at[kind, 1, 1], to_left)

    y_state = {}
    for way in (True, False):
        for kind in kinds:
            go_up = upward[kind] == way
            y_state[kind, go_up] = links.send(own_refs[kind], all_refs[kind].at[ep, tp], to_up if go_up else to_down)
    groups = (tp, down, up, over)
    states = [spread(tp, own_refs)]
    hold = [pltpu.make_async_copy(own_refs[kind], all_refs[kind].at[ep, tp], row_sem.at[kind]) for kind in range(3)]
    for copy in hold:
        copy.start()
    for copy in loads:
        copy.wait()
    stow = [pltpu.make_async_copy(w13, w13_all.at[tp], w_sem.at[0]), pltpu.make_async_copy(w2s, w2_all.at[tp], w_sem.at[1])]
    for copy in stow:
        copy.start()
    earlier[...] = earlier_rows(earlier.shape[0])
    acc13[...] = jnp.zeros_like(acc13)
    acc2[...] = jnp.zeros_like(acc2)

    def y_arrive(kind, way):
        block = all_refs[kind].at[ep, down if way else up]
        links.arrive(y_state[kind, way], block, to_up if way else to_down)
        return block

    for kind in kinds:
        block = y_arrive(kind, upward[kind])
        y_state[kind, "far"] = links.send(block, block, to_up if upward[kind] else to_down)
    pass_on(0)
    for kind in kinds:
        y_arrive(kind, not upward[kind])
    send_weights(0)
    send_weights(1)
    for g in (1, 2):
        states.append(spread(groups[g], [ref.at[ep, groups[g]] for ref in all_refs]))
    share(0)
    last(0)
    for kind in kinds:
        links.arrive(y_state[kind, "far"], all_refs[kind].at[ep, over], to_up if upward[kind] else to_down)
    for copy in hold + stow:
        copy.wait()
    from_mate(0)
    route_copy = pltpu.make_async_copy(r_all.at[:, tp], routes, row_sem.at[0])
    route_copy.start()
    route_copy.wait()
    compute(tp, True)

    pass_on(1)
    states.append(spread(over, [ref.at[ep, over] for ref in all_refs]))
    pass_weights(0)
    send_weights(2)
    share(1)
    pass_on(2)
    pass_weights(1)
    send_weights(3)
    expert(0)
    share(2)
    last(1)
    from_mate(1)
    compute(groups[1], False)
    pass_weights(2)
    send_weights(4)
    pass_on(3)
    expert(1)
    share(3)
    pass_weights(3)
    last(2)
    from_mate(2)
    expert(2)
    last(3)
    compute(groups[2], False)
    pass_weights(4)
    expert(3)
    have_weights(4)
    copies = fetch(4)
    forward(4, copies)
    y_sum = sum_up(0)
    backward(4, copies)
    dx_sum = sum_up(1)
    turn_sums(0, y_sum)
    from_mate(3)
    compute(groups[3], False)
    turn_sums(1, dx_sum)

    def finish(e, carry):
        g_buf[0] = acc13[e, :width, :].T.astype(BF16)
        g_buf[1] = acc13[e, width:, :].T.astype(BF16)
        copies = [pltpu.make_async_copy(g_buf.at[0], g1.at[e], g_sem.at[0]), pltpu.make_async_copy(g_buf.at[1], g3.at[e], g_sem.at[1])]
        xs[0, pl.ds(0, width), :] = acc2[e].astype(BF16)
        copies.append(pltpu.make_async_copy(xs.at[0, pl.ds(0, width)], g2.at[e], g_sem.at[2]))
        for copy in copies:
            copy.start()
        for copy in copies:
            copy.wait()
        return carry

    lax.fori_loop(0, own, finish, 0)
    sums_here(0, y_sum)
    sums_here(1, dx_sum)
    links.drain()


def layer(tokens, d_out, routes, w_one, w_three, w_two, ep_size, tp_size, cap):
    tok, model = tokens.shape
    own, width, _ = w_two.shape
    half = ep_size // 2
    rows = half * cap
    side = model // 2
    vmem, hbm = pl.BlockSpec(memory_space=pltpu.VMEM), pl.BlockSpec(memory_space=pl.ANY)
    shape = jax.ShapeDtypeStruct
    copies = copy_count(own)
    slot_rows = ep_size * tp_size * cap * own
    vector = pltpu.VMEM
    dma = pltpu.SemaphoreType.DMA
    outs = pl.pallas_call(
        functools.partial(layer_kernel, own, cap, width),
        in_specs=[vmem, vmem, vmem, hbm, hbm, hbm],
        out_specs=[hbm] * 15,
        out_shape=[
            shape((ep_size, tp_size, tok, model), BF16),
            shape((ep_size, tp_size, tok, model), BF16),
            shape((ep_size, tp_size) + routes.shape, F32),
            shape((tp_size, own, model, 2 * width), BF16),
            shape((tp_size, own, width, model), BF16),
            shape((own, 2, rows, model), BF16),
            shape((own, 2, rows, model), BF16),
            shape((2, ep_size, own, cap, model), BF16),
            shape((2, 4, 2, tok, side), F32),
            shape((2, 4, 2, tok, side), F32),
            shape((2, 2, tok, side), F32),
            shape((2, 2, 2, tok, side), F32),
            shape((own, model, width), BF16),
            shape((own, model, width), BF16),
            shape((own, width, model), BF16),
        ],
        scratch_shapes=[
            vector((own, model, 2 * width), BF16),
            vector((own, width, model), BF16),
            vector((2, half // 2, tok, model), BF16),
            vector((2, half // 2, tok, model), BF16),
            vector((2, half // 2) + routes.shape, F32),
            vector((ep_size,) + routes.shape, F32),
            vector((tok, tok), BF16),
            vector((own, rows, model), BF16),
            vector((own, rows, model), BF16),
            vector((own, 2 * width, model), F32),
            vector((own, width, model), F32),
            vector((2, model, width), BF16),
            vector((tp_size, model, 2 * width), BF16),
            vector((tp_size, width, model), BF16),
            vector((tp_size, 2 * rows, 2 * width), F32),
            vector((2 * rows, tp_size * width), BF16),
            vector((tp_size, 2 * rows, 2 * width), BF16),
            vector((ep_size, cap, model), BF16),
            vector((ep_size, cap, model), BF16),
            vector((2, own, cap, model), BF16),
            vector((3, own * cap, tok), BF16),
            vector((2, 2, tok, side), F32),
            vector((2, 2, tok, side), F32),
            vector((2, tok, side), F32),
            vector((2, 2, tok, side), F32),
            dma((copies,)),
            dma((copies,)),
            dma((3,)),
            dma((3, 2)),
            dma((3,)),
            dma((2,)),
            dma((3 + tp_size,)),
            dma((2,)),
            dma((2,)),
            dma((3,)),
            dma((3,)),
        ],
        compiler_params=pltpu.CompilerParams(vmem_limit_bytes=VMEM_LIMIT, collective_id=0, has_side_effects=True),
        cost_estimate=pl.CostEstimate(
            flops=2 * slot_rows * model * (2 * tok + 12 * width),
            bytes_accessed=4 * ep_size * tp_size * tok * model,
            transcendentals=0,
        ),
        name="layer",
    )(tokens, d_out, routes, w_one, w_three, w_two)
    return outs[8], outs[11], outs[12:]


def result_kernel(sums, last_land, g1, g3, g2, out, dx, o1, o3, o2, parts, rows, b1, b3, b2, in_sem, out_sem):
    grads = ((g1, b1, o1), (g3, b3, o3), (g2, b2, o2))
    takes = [pltpu.make_async_copy(src, buf, in_sem.at[k]) for k, (src, buf, _) in enumerate(grads)]
    terms = [[pltpu.make_async_copy(sums.at[kind, 3], parts.at[kind, 2], in_sem.at[3 + kind]),
              pltpu.make_async_copy(last_land.at[kind], parts.at[kind, pl.ds(0, 2)], in_sem.at[5 + kind])] for kind in range(2)]
    for copy in terms[0] + terms[1] + takes:
        copy.start()
    puts = []
    side = parts.shape[4]
    for kind, to in ((0, out), (1, dx)):
        for copy in terms[kind]:
            copy.wait()
        for s in range(2):
            total = parts[kind, 2, s] + (parts[kind, 0, s] + parts[kind, 1, s])
            rows[kind, :, s * side : (s + 1) * side] = total.astype(BF16)
        puts.append(pltpu.make_async_copy(rows.at[kind], to, out_sem.at[3 + kind]))
        puts[-1].start()
    for k, (take, (_, buf, to)) in enumerate(zip(takes, grads)):
        take.wait()
        puts.append(pltpu.make_async_copy(buf, to, out_sem.at[k]))
        puts[-1].start()
    for copy in puts:
        copy.wait()


def results(sums, last_land, grads):
    _, _, _, tok, side = sums.shape
    hbm = pl.BlockSpec(memory_space=pl.ANY)
    row = jax.ShapeDtypeStruct((tok, 2 * side), BF16)
    return pl.pallas_call(
        result_kernel,
        in_specs=[hbm] * 5,
        out_specs=[hbm] * 5,
        out_shape=[row, row] + [jax.ShapeDtypeStruct(g.shape, g.dtype) for g in grads],
        scratch_shapes=[pltpu.VMEM((2, 3, 2, tok, side), F32), pltpu.VMEM((2, tok, 2 * side), BF16)]
        + [pltpu.VMEM(g.shape, g.dtype) for g in grads]
        + [pltpu.SemaphoreType.DMA((7,)), pltpu.SemaphoreType.DMA((5,))],
        compiler_params=pltpu.CompilerParams(vmem_limit_bytes=VMEM_LIMIT),
        name="results",
    )(sums, last_land, *grads)


def solution(mesh):
    ep_size, tp_size = mesh.shape["ep"], mesh.shape["tp"]
    row_spec = P(("dp", "ep", "tp"), None)
    col_spec = P("ep", None, "tp")
    down_spec = P("ep", "tp", None)
    grad_col = P(("dp", "ep"), None, "tp")
    grad_down = P(("dp", "ep"), "tp", None)

    def local_step(tokens, expert_ids, gate_vals, w_one, w_three, w_two, d_out):
        cap = slot_count(expert_ids.shape[1], tokens.shape[0], w_one.shape[0] * ep_size)
        routes = jnp.concatenate([expert_ids.T.astype(F32), gate_vals.T], axis=0)
        sums, last_land, grads = layer(tokens, d_out, routes, w_one, w_three, w_two, ep_size, tp_size, cap)
        return tuple(results(sums, last_land, grads))

    return jax.shard_map(local_step, mesh=mesh,
                         in_specs=(row_spec, row_spec, row_spec, col_spec, col_spec, down_spec, row_spec),
                         out_specs=(row_spec, row_spec, grad_col, grad_col, grad_down), check_vma=False)
```

time: 2050 us -> 384 us (0.19)
  waiting for transfers between devices: 1450 us -> 0 us
  Pallas kernels: 0 us -> 381 us
  matrix products: 198 us -> 0 us
  blocking collectives: 187 us -> 0 us
  local copies, waits for them, and re-layouts: 128 us -> 0 us
  other arithmetic: 54.4 us -> 2 us
    reduce_scatter x2 -> x0, waiting for transfers between devices: 984 us -> none  [the longest x1 493 us: local_step(): lax.psum_scatter(part_dx, 'tp', scatter_dimension=1, tiled=True)]
    all_gather x2 -> x0, waiting for transfers between devices: 390 us -> none  [the longest x1 243 us: local_step(): rows_grad = lax.all_gather(recv_grad, 'tp', axis=1, tiled=True)]
    pallas_call x0 -> x2, Pallas kernels: none -> 381 us  [the longest x1 372 us: layer(): pl.pallas_call(functools.partial(layer_kernel, own, cap, width), in_specs...]
    dot_general x9 -> x0, matrix products: 198 us -> none  [the longest x1 45.3 us: local_step(): jnp.einsum('enf,edf->end', d_three, w_three, preferred_element_type=jnp.f...]
    all_to_all x2 -> x0, blocking collectives: 187 us -> none  [the longest x1 93.8 us: local_step(): recv_in = lax.all_to_all(slot_in, 'ep', 0, 1, tiled=True)]
    all_to_all x2 -> x0, waiting for transfers between devices: 76.2 us -> none  [the longest x1 76.2 us: local_step(): lax.all_to_all(mine_out, 'ep', 1, 0, tiled=True)]
    gather x4 -> x0, local copies, waits for them, and re-layouts: 64.9 us -> none  [take_rows(): return jnp.take(source, index_list, axis=0, mode='fill', fill_value=0)]
    all_to_all x4 -> x0, local copies, waits for them, and re-layouts: 29.1 us -> none  [the longest x1 11 us: local_step(): lax.all_to_all(mine_out, 'ep', 1, 0, tiled=True)]
  transfers between devices with their start and end apart: 6 -> 0, of which waited for: 5 -> 0; matrix products, arithmetic and copies ran while one was open for 10% -> 0% of each run, Pallas kernels for 0% -> 0%
where the time goes in v3:
time: 384 us; the launch traced here: 383 us
  Pallas kernels  381 us (99%)
    pallas_call x1, Pallas kernels, layer(): pl.pallas_call(functools.partial(layer_kernel, own, cap, width), in_specs...  372 us
    pallas_call x1, Pallas kernels, results(): pl.pallas_call(result_kernel, in_specs=[hbm] * 5, out_specs=[hbm] * 5, ou...  8.22 us

profile of v3, /device:TPU:97, one launch (start us, length us, event | category | flops | bytes accessed | tf_op | source)
XLA Modules:
  0.0 383.4 jit_solution(924045992528188092)
XLA Ops:
  0.6 0.7 convert_bitcast_fusion
  1.3 1.3 pad_maximum_fusion.r_own
  2.6 372.3 %layer.1 = (bf16[8,4,256,1536]{3,2,1,0:T(8,128)(2,1)}, bf16[8,4,256,1536]{3,2,1,0:T(8,128)(2,1)}, f32[8,4,16,256]{3,2,1,0:T(8,128)}, bf16[4,5,1536,256]{3,2,1,0:...) custom-call(bf16[256,1536]{1,0:T(8,128)(2,1)} %x_own.1, ...), custom_call_target="tpu_custom_call" | custom-call | flops 64424509440 | bytes 50331648 | tf_op jit(solution)/shard_map/layer/pallas_call | solution.py:558
  375.0 8.2 %results.1 = (bf16[256,1536]{1,0:T(8,128)(2,1)}, bf16[256,1536]{1,0:T(8,128)(2,1)}, bf16[5,1536,128]{2,1,0:T(8,128)(2,1)}, bf16[5,1536,128]{2,1,0:T(8,128)(2,1)}, bf16[5,128,1536]{2,1,0:T(8,128)(2,1)}) custom-call(f32[2,4,2,256,768]{4,3,2,1,0:T(8,128)} %get-tuple-element.10.sums, f32[2,2,2,256,768]{4,3,2,1,0:T(8,128)} %get-tuple-element.11.last_land, ...), custom_call_target="tpu_custom_call" | custom-call | tf_op jit(solution)/shard_map/results/pallas_call | solution.py:657

commit v4 on v3

--- a/solution.py
+++ b/solution.py
@@ -93,7 +93,7 @@
 
 
 def copy_count(own):
-    return 9 + 21 * 4 + 7 * own + 2 * 10
+    return 6 + 21 * 3 + 24 + 7 * own + 2 * 10
 
 
 def layer_kernel(own, cap, width, x_own, dy_own, r_own, w1, w3, w2, x_all, dy_all, r_all, w13_all, w2_all, xs_all, us_all,
@@ -174,6 +174,23 @@
             for name, at in (("mate", mate), ("mate1", one), ("mate2", two), ("mate3", mate_step(4))):
                 links.arrive(state[kind, name], all_refs[kind].at[at, t], to_mate)
 
+    core = lax.rem(ep, 2)
+
+    def send_over():
+        return [{kind: links.send(all_refs[kind].at[core + 2 * m, down if upward[kind] else up],
+                                  all_refs[kind].at[core + 2 * m, down if upward[kind] else up],
+                                  to_up if upward[kind] else to_down) for kind in kinds} for m in range(half)]
+
+    def share_over(m):
+        for kind in kinds:
+            block = all_refs[kind].at[core + 2 * m, over]
+            links.arrive(over_state[m][kind], block, to_up if upward[kind] else to_down)
+            over_state[m][kind, "mate"] = links.send(block, block, to_mate)
+
+    def have_over(m):
+        for kind in kinds:
+            links.arrive(over_state[m][kind, "mate"], all_refs[kind].at[1 - core + 2 * m, over], to_mate)
+
     cut = 3 * model // 4
     w_state = [None] * own
 
@@ -204,63 +221,69 @@
         return [pltpu.make_async_copy(src.at[at, t], dst.at[p], load_sem.at[k, p])
                 for k, (src, dst) in enumerate(((x_all, xb), (dy_all, dyb), (r_all, rb)))]
 
+    def half_group(t, h, keep, ahead):
+        for p in range(2):
+            for copy in pair_loads(t, h, p):
+                copy.wait()
+
+            def gather(b, carry):
+                pos, gate = expert_rows(rb[p, b], ep * own, own, earlier[...])
+                masks = hit_masks(pos, cap)
+                pick = one_hot(masks)
+                gates = jnp.sum(slot_gates(masks, gate), axis=1, keepdims=True)
+                rows = pl.ds(pl.multiple_of((p * (half // 2) + b) * cap, cap), cap)
+                picked = dot(pick, xb[p, b]).astype(BF16)
+                for e in range(own):
+                    xs[e, rows, :] = picked[e * cap : (e + 1) * cap]
+                scaled = (gates * dot(pick, dyb[p, b])).astype(BF16)
+                for e in range(own):
+                    us[e, rows, :] = scaled[e * cap : (e + 1) * cap]
+                return carry
+
+            lax.fori_loop(0, half // 2, gather, 0)
+
+            @pl.when(ahead)
+            def _():
+                for copy in pair_loads(t, 1, p):
+                    copy.start()
+
+        stores = []
+        if keep:
+            stores = [pltpu.make_async_copy(xs, xs_all.at[:, h], slot_sem.at[0]),
+                      pltpu.make_async_copy(us, us_all.at[:, h], slot_sem.at[1])]
+        for copy in stores:
+            copy.start()
+
+        def expert(e, carry):
+            ab = dot(xs[e], w13[e])
+            a, b = ab[:, :width], ab[:, width:]
+            dh = dot_tb(us[e], w2s[e])
+            sig = jax.nn.sigmoid(a)
+            silu = a * sig
+            hid = (silu * b).astype(BF16)
+            da = (dh * b * sig * (1.0 + a * (1.0 - sig))).astype(BF16)
+            db = (dh * silu).astype(BF16)
+            acc13[e] += dot_ta(jnp.concatenate([da, db], axis=1), xs[e])
+            acc2[e] += dot_ta(hid, us[e])
+            return carry
+
+        lax.fori_loop(0, own, expert, 0)
+        for copy in stores:
+            copy.wait()
+
+    def start_loads(t, h):
+        for p in range(2):
+            for copy in pair_loads(t, h, p):
+                copy.start()
+
     def compute(t, keep):
-        for p in range(2):
-            for copy in pair_loads(t, 0, p):
-                copy.start()
-
-        def half_group(h, carry):
-            for p in range(2):
-                for copy in pair_loads(t, h, p):
-                    copy.wait()
-
-                def gather(b, carry):
-                    pos, gate = expert_rows(rb[p, b], ep * own, own, earlier[...])
-                    masks = hit_masks(pos, cap)
-                    pick = one_hot(masks)
-                    gates = jnp.sum(slot_gates(masks, gate), axis=1, keepdims=True)
-                    rows = pl.ds(pl.multiple_of((p * (half // 2) + b) * cap, cap), cap)
-                    picked = dot(pick, xb[p, b]).astype(BF16)
-                    for e in range(own):
-                        xs[e, rows, :] = picked[e * cap : (e + 1) * cap]
-                    scaled = (gates * dot(pick, dyb[p, b])).astype(BF16)
-                    for e in range(own):
-                        us[e, rows, :] = scaled[e * cap : (e + 1) * cap]
-                    return carry
-
-                lax.fori_loop(0, half // 2, gather, 0)
-
-                @pl.when(h == 0)
-                def _():
-                    for copy in pair_loads(t, 1, p):
-                        copy.start()
-
-            stores = []
-            if keep:
-                stores = [pltpu.make_async_copy(xs, xs_all.at[:, h], slot_sem.at[0]),
-                          pltpu.make_async_copy(us, us_all.at[:, h], slot_sem.at[1])]
-            for copy in stores:
-                copy.start()
-
-            def expert(e, carry):
-                ab = dot(xs[e], w13[e])
-                a, b = ab[:, :width], ab[:, width:]
-                dh = dot_tb(us[e], w2s[e])
-                sig = jax.nn.sigmoid(a)
-                silu = a * sig
-                hid = (silu * b).astype(BF16)
-                da = (dh * b * sig * (1.0 + a * (1.0 - sig))).astype(BF16)
-                db = (dh * silu).astype(BF16)
-                acc13[e] += dot_ta(jnp.concatenate([da, db], axis=1), xs[e])
-                acc2[e] += dot_ta(hid, us[e])
-                return carry
-
-            lax.fori_loop(0, own, expert, 0)
-            for copy in stores:
-                copy.wait()
+        start_loads(t, 0)
+
+        def one_half(h, carry):
+            half_group(t, h, keep, h == 0)
             return carry
 
-        lax.fori_loop(0, 2, half_group, 0)
+        lax.fori_loop(0, 2, one_half, 0)
 
     def fetch(e):
         copies = [pltpu.make_async_copy(xs_all.at[e], xs.at[pl.ds(0, 2)], in_sem.at[0]),
@@ -353,13 +376,17 @@
         for k, part in enumerate(parts):
             gates_buf[k] = part
         row_load(kind, block, slot).wait()
-        for s in range(2):
+
+        def one_side(s, carry):
+            rows = c_buf[slot, :, :, pl.ds(pl.multiple_of(s * side, side), side)].reshape(own * cap, side)
             total = None
-            rows = c_buf[slot, :, :, s * side : (s + 1) * side].reshape(own * cap, side)
             for k in reversed(range(len(parts))):
                 term = dot_ta(gates_buf[k], rows)
                 total = term if total is None else total + term
             tile[s] = total
+            return carry
+
+        lax.fori_loop(0, 2, one_side, 0)
 
     def sum_up(kind):
         settle_rows(kind)
@@ -447,7 +474,7 @@
         for kind in kinds:
             go_up = upward[kind] == way
             y_state[kind, go_up] = links.send(own_refs[kind], all_refs[kind].at[ep, tp], to_up if go_up else to_down)
-    groups = (tp, down, up, over)
+    groups = (tp, down, up)
     states = [spread(tp, own_refs)]
     hold = [pltpu.make_async_copy(own_refs[kind], all_refs[kind].at[ep, tp], row_sem.at[kind]) for kind in range(3)]
     for copy in hold:
@@ -466,20 +493,16 @@
         links.arrive(y_state[kind, way], block, to_up if way else to_down)
         return block
 
-    for kind in kinds:
-        block = y_arrive(kind, upward[kind])
-        y_state[kind, "far"] = links.send(block, block, to_up if upward[kind] else to_down)
     pass_on(0)
-    for kind in kinds:
-        y_arrive(kind, not upward[kind])
+    for way in (True, False):
+        for kind in kinds:
+            y_arrive(kind, way)
     send_weights(0)
     send_weights(1)
     for g in (1, 2):
         states.append(spread(groups[g], [ref.at[ep, groups[g]] for ref in all_refs]))
     share(0)
     last(0)
-    for kind in kinds:
-        links.arrive(y_state[kind, "far"], all_refs[kind].at[ep, over], to_up if upward[kind] else to_down)
     for copy in hold + stow:
         copy.wait()
     from_mate(0)
@@ -488,42 +511,49 @@
     route_copy.wait()
     compute(tp, True)
 
-    pass_on(1)
-    states.append(spread(over, [ref.at[ep, over] for ref in all_refs]))
     pass_weights(0)
     send_weights(2)
+    pass_on(1)
     share(1)
-    pass_on(2)
     pass_weights(1)
     send_weights(3)
     expert(0)
+    pass_on(2)
     share(2)
+    pass_weights(2)
+    send_weights(4)
     last(1)
     from_mate(1)
+    expert(1)
+    last(2)
     compute(groups[1], False)
-    pass_weights(2)
-    send_weights(4)
-    pass_on(3)
-    expert(1)
-    share(3)
     pass_weights(3)
-    last(2)
+    expert(2)
     from_mate(2)
-    expert(2)
-    last(3)
     compute(groups[2], False)
     pass_weights(4)
+    over_state = send_over()
     expert(3)
-    have_weights(4)
-    copies = fetch(4)
-    forward(4, copies)
+    have_weights(own - 1)
+    copies = fetch(own - 1)
+    forward(own - 1, copies)
     y_sum = sum_up(0)
-    backward(4, copies)
+    share_over(0)
+    backward(own - 1, copies)
     dx_sum = sum_up(1)
     turn_sums(0, y_sum)
-    from_mate(3)
-    compute(groups[3], False)
+    share_over(1)
+    have_over(0)
+    have_over(1)
+    start_loads(over, 0)
+    half_group(over, 0, False, False)
+    share_over(2)
     turn_sums(1, dx_sum)
+    share_over(3)
+    have_over(2)
+    have_over(3)
+    start_loads(over, 1)
+    half_group(over, 1, False, False)
 
     def finish(e, carry):
         g_buf[0] = acc13[e, :width, :].T.astype(BF16)

time: 384 us -> 370 us (0.964)
  Pallas kernels: 381 us -> 367 us
    pallas_call x1, Pallas kernels: 372 us -> 359 us  [layer(): pl.pallas_call(functools.partial(layer_kernel, own, cap, width), in_specs...]
where the time goes in v4:
time: 370 us
  Pallas kernels  367 us (99%)
    pallas_call x1, Pallas kernels, layer(): pl.pallas_call(functools.partial(layer_kernel, own, cap, width), in_specs...  359 us
    pallas_call x1, Pallas kernels, results(): pl.pallas_call(result_kernel, in_specs=[hbm] * 5, out_specs=[hbm] * 5, ou...  8.22 us

profile of v4, /device:TPU:97, one launch (start us, length us, event | category | flops | bytes accessed | tf_op | source)
XLA Modules:
  0.0 369.6 jit_solution(3492486876034161251)
XLA Ops:
  0.6 0.7 convert_bitcast_fusion
  1.3 1.3 pad_maximum_fusion.r_own
  2.6 358.5 %layer.1 = (bf16[8,4,256,1536]{3,2,1,0:T(8,128)(2,1)}, bf16[8,4,256,1536]{3,2,1,0:T(8,128)(2,1)}, f32[8,4,16,256]{3,2,1,0:T(8,128)}, bf16[4,5,1536,256]{3,2,1,0:...) custom-call(bf16[256,1536]{1,0:T(8,128)(2,1)} %x_own.1, ...), custom_call_target="tpu_custom_call" | custom-call | flops 64424509440 | bytes 50331648 | tf_op jit(solution)/shard_map/layer/pallas_call | solution.py:588
  361.2 8.2 %results.1 = (bf16[256,1536]{1,0:T(8,128)(2,1)}, bf16[256,1536]{1,0:T(8,128)(2,1)}, bf16[5,1536,128]{2,1,0:T(8,128)(2,1)}, bf16[5,1536,128]{2,1,0:T(8,128)(2,1)}, bf16[5,128,1536]{2,1,0:T(8,128)(2,1)}) custom-call(f32[2,4,2,256,768]{4,3,2,1,0:T(8,128)} %get-tuple-element.10.sums, f32[2,2,2,256,768]{4,3,2,1,0:T(8,128)} %get-tuple-element.11.last_land, ...), custom_call_target="tpu_custom_call" | custom-call | tf_op jit(solution)/shard_map/results/pallas_call | solution.py:687

commit v5 on v4

--- a/solution.py
+++ b/solution.py
@@ -93,12 +93,12 @@
 
 
 def copy_count(own):
-    return 6 + 21 * 3 + 24 + 7 * own + 2 * 10
-
-
-def layer_kernel(own, cap, width, x_own, dy_own, r_own, w1, w3, w2, x_all, dy_all, r_all, w13_all, w2_all, xs_all, us_all,
-                 ys_all, sums, mate_land, half_land, last_land, g1, g3, g2, w13, w2s, xb, dyb, rb, routes, earlier, xs, us,
-                 acc13, acc2, g_buf, w13e, w2e, ab_buf, h_buf, d_buf, y_buf, v_buf, c_buf, gates_buf, give, keep_sum, mate_sum,
+    return 6 + 21 * 3 + 24 + 7 * own + 2 * 10 + 1
+
+
+def layer_kernel(own, cap, width, tokens, d_out, ids, gate_vals, w1, w3, w2, x_all, dy_all, r_all, w13_all, w2_all, xs_all, us_all,
+                 ys_all, sums, mate_land, half_land, last_land, out, g1, g3, g2, x_own, dy_own, r_own, i_own, far_gates, w13, w2s, xb, dyb, rb, routes, earlier, xs, us,
+                 acc13, acc2, g_buf, w13e, w2e, ab_buf, h_buf, d_buf, y_buf, v_buf, c_buf, gates_buf, give, keep_sum, far_sum, mate_sum,
                  turn_sum, send_sem, recv_sem, row_sem, load_sem, w_sem, slot_sem, in_sem, out_sem, c_sem, sum_sem, g_sem):
     ep, tp = lax.axis_index("ep"), lax.axis_index("tp")
     eps, tps = x_all.shape[0], x_all.shape[1]
@@ -116,20 +116,27 @@
     links = Links(send_sem, recv_sem)
     wide = 512 if model % 512 == 0 else model
 
+    barrier = pltpu.get_barrier_semaphore()
+    for to in (to_right, to_left, to_mate, to_up, to_down):
+        pl.semaphore_signal(barrier, inc=1, device_id=to, device_id_type=MESH)
+    top = ids.shape[0]
+    firsts = [pltpu.make_async_copy(ids, i_own, row_sem.at[0]), pltpu.make_async_copy(gate_vals, r_own.at[pl.ds(top, top)], row_sem.at[1]),
+              pltpu.make_async_copy(tokens, x_own, row_sem.at[2]), pltpu.make_async_copy(d_out, dy_own, row_sem.at[3])]
     loads = [pltpu.make_async_copy(w1, w13.at[:, :, pl.ds(0, width)], w_sem.at[0]),
              pltpu.make_async_copy(w3, w13.at[:, :, pl.ds(width, width)], w_sem.at[1]),
              pltpu.make_async_copy(w2, w2s, w_sem.at[2])]
-    for copy in loads:
+    for copy in firsts + loads:
         copy.start()
-
-    barrier = pltpu.get_barrier_semaphore()
-    for to in (to_right, to_left, to_mate, to_up, to_down):
-        pl.semaphore_signal(barrier, inc=1, device_id=to, device_id_type=MESH)
-    pl.semaphore_wait(barrier, 5)
+    firsts[0].wait()
+    r_own[0:top] = i_own[...].astype(F32)
+    for copy in firsts[1:]:
+        copy.wait()
+    with jax.named_scope("barrier"):
+        pl.semaphore_wait(barrier, 5)
 
     own_refs, all_refs = (x_own, dy_own, r_own), (x_all, dy_all, r_all)
     upward = (True, False, True)
-    kinds = (0, 2, 1)
+    kinds = (0, 1, 2)
 
     def spread(t, srcs):
         out = {}
@@ -285,14 +292,20 @@
 
         lax.fori_loop(0, 2, one_half, 0)
 
+    def fetch_rows(e):
+        copies = [pltpu.make_async_copy(xs_all.at[e], xs.at[pl.ds(0, 2)], in_sem.at[0]),
+                  pltpu.make_async_copy(us_all.at[e], us.at[pl.ds(0, 2)], in_sem.at[1])]
+        for copy in copies:
+            copy.start()
+        return copies
+
     def fetch(e):
-        copies = [pltpu.make_async_copy(xs_all.at[e], xs.at[pl.ds(0, 2)], in_sem.at[0]),
-                  pltpu.make_async_copy(us_all.at[e], us.at[pl.ds(0, 2)], in_sem.at[1]),
-                  pltpu.make_async_copy(w2_all.at[:, e], w2e, in_sem.at[2])]
-        copies += [pltpu.make_async_copy(w13_all.at[j, e], w13e.at[j], in_sem.at[3 + j]) for j in range(tps)]
-        for k in (0, 3, 4, 5, 6, 2, 1):
-            copies[k].start()
-        return copies
+        copies = fetch_rows(e)
+        weights = [pltpu.make_async_copy(w13_all.at[j, e], w13e.at[j], in_sem.at[3 + j]) for j in range(tps)]
+        weights.append(pltpu.make_async_copy(w2_all.at[:, e], w2e, in_sem.at[2]))
+        for copy in weights:
+            copy.start()
+        return copies + weights[-1:]
 
     slots = eps * cap
     pending = {}
@@ -310,19 +323,14 @@
         if kind in pending:
             pending.pop(kind).wait()
 
-    def forward(e, copies):
-        copies[0].wait()
-
-        def shard(j, carry):
-            pltpu.make_async_copy(w13_all.at[j, e], w13e.at[j], in_sem.at[3 + j]).wait()
-            ab = dot(xs[0:2].reshape(slots, model), w13e[j])
-            ab_buf[j] = ab
-            a, b = ab[:, :width], ab[:, width:]
-            h_buf[:, pl.ds(pl.multiple_of(j * width, width), width)] = (a * jax.nn.sigmoid(a) * b).astype(BF16)
-            return carry
-
-        lax.fori_loop(0, tps, shard, 0)
-        copies[2].wait()
+    def hidden(e, j):
+        pltpu.make_async_copy(w13_all.at[j, e], w13e.at[j], in_sem.at[3 + j]).wait()
+        ab = dot(xs[0:2].reshape(slots, model), w13e[j])
+        ab_buf[j] = ab
+        a, b = ab[:, :width], ab[:, width:]
+        h_buf[:, pl.ds(pl.multiple_of(j * width, width), width)] = (a * jax.nn.sigmoid(a) * b).astype(BF16)
+
+    def rows_out(e):
         settle_rows(0)
 
         def columns(n, carry):
@@ -332,6 +340,38 @@
 
         lax.fori_loop(0, model // wide, columns, 0)
         store_rows(0, y_buf, e)
+
+    def forward(e, copies):
+        copies[0].wait()
+
+        def shard(j, carry):
+            hidden(e, j)
+            return carry
+
+        lax.fori_loop(0, tps, shard, 0)
+        copies[2].wait()
+        rows_out(e)
+
+    def forward_early(e):
+        copies = fetch_rows(e)
+        for j in (tp, up, down):
+            pltpu.make_async_copy(w13_all.at[j, e], w13e.at[j], in_sem.at[3 + j]).start()
+        copies[0].wait()
+
+        def shard(i, carry):
+            hidden(e, lax.rem(tp + i + i // 2, tps))
+            return carry
+
+        lax.fori_loop(0, tps - 1, shard, 0)
+        return copies
+
+    def forward_late(e):
+        pltpu.make_async_copy(w13_all.at[over, e], w13e.at[over], in_sem.at[3 + over]).start()
+        w2_copy = pltpu.make_async_copy(w2_all.at[:, e], w2e, in_sem.at[2])
+        w2_copy.start()
+        hidden(e, over)
+        w2_copy.wait()
+        rows_out(e)
 
     def backward(e, copies):
         copies[1].wait()
@@ -366,50 +406,124 @@
 
     offsets = (4, 2, -2, 0)
 
-    def row_load(kind, block, slot):
-        return pltpu.make_async_copy(ys_all.at[kind, block], c_buf.at[slot], c_sem.at[slot])
-
-    def combine(kind, block, slot, tile):
+    def row_load(kind, block, slot, first=0, count=None):
+        part = pl.ds(first, own if count is None else count)
+        return pltpu.make_async_copy(ys_all.at[kind, block, part], c_buf.at[slot, part], c_sem.at[slot])
+
+    def block_parts(kind, block, parts):
         pos, gate = expert_rows(routes[block], ep * own, own, earlier[...])
         masks = hit_masks(pos, cap)
-        parts = three_parts(slot_gates(masks, gate)) if kind == 0 else (one_hot(masks),)
-        for k, part in enumerate(parts):
-            gates_buf[k] = part
+        for k, part in enumerate(three_parts(slot_gates(masks, gate)) if kind == 0 else (one_hot(masks),)):
+            parts[k] = part
+
+    def gated(parts, count, first, rows):
+        total = None
+        for k in reversed(range(count)):
+            term = dot_ta(parts[k, first : first + rows.shape[0]], rows)
+            total = term if total is None else total + term
+        return total
+
+    def columns_of(s):
+        return pl.ds(pl.multiple_of(s * side, side), side)
+
+    def combine(kind, block, slot, tile):
+        block_parts(kind, block, gates_buf)
         row_load(kind, block, slot).wait()
 
         def one_side(s, carry):
-            rows = c_buf[slot, :, :, pl.ds(pl.multiple_of(s * side, side), side)].reshape(own * cap, side)
-            total = None
-            for k in reversed(range(len(parts))):
-                term = dot_ta(gates_buf[k], rows)
-                total = term if total is None else total + term
-            tile[s] = total
+            tile[s] = gated(gates_buf, 3 if kind == 0 else 1, 0, c_buf[slot, :, :, columns_of(s)].reshape(own * cap, side))
             return carry
 
         lax.fori_loop(0, 2, one_side, 0)
 
+    early = own - 2
+    far_blocks = (mate_step(4), far)
+    far_tiles = (give.at[0], far_sum)
+
+    def combine_early():
+        for slot, block in enumerate(far_blocks):
+            row_load(0, block, slot, 0, early).start()
+        for slot, block in enumerate(far_blocks):
+            block_parts(0, block, far_gates.at[slot])
+            row_load(0, block, slot, 0, early).wait()
+
+            def one_side(s, carry):
+                rows = c_buf[slot, 0:early, :, columns_of(s)].reshape(early * cap, side)
+                far_tiles[slot][s] = gated(far_gates.at[slot], 3, 0, rows)
+                return carry
+
+            lax.fori_loop(0, 2, one_side, 0)
+
+    def load_next():
+        settle_rows(0)
+        for slot, block in enumerate(far_blocks):
+            row_load(0, block, slot, early, 1).start()
+
+    def combine_late(slot, s):
+        block = far_blocks[slot]
+        rows = jnp.concatenate([c_buf[slot, early, :, columns_of(s)], y_buf[block, :, columns_of(s)]], axis=0)
+        far_tiles[slot][s] += gated(far_gates.at[slot], 3, early * cap, rows)
+
     def sum_up(kind):
-        settle_rows(kind)
         state = {}
-        blocks = [(mate_step(o), step(o)) for o in offsets]
-        order = [b for pair in blocks for b in pair]
-        row_load(kind, order[0], 0).start()
+        order = [b for o in offsets for b in (mate_step(o), step(o))]
 
         def one(n, tile):
             if n + 1 < len(order):
                 row_load(kind, order[n + 1], (n + 1) % 2).start()
             combine(kind, order[n], n % 2, tile)
 
-        gifts, writes = [], []
+        gifts, writes = [], [None]
 
         def give_block(i):
             if i >= 2:
-                links.finish(gifts[i - 2])
+                if i > 2 or kind == 1:
+                    links.finish(gifts[i - 2])
+                else:
+                    for k in gifts[0]:
+                        links.finish(k)
             one(2 * i, give.at[i % 2])
             gifts.append(links.send(give.at[i % 2], mate_land.at[kind, i], to_mate))
 
         def own_block(i):
             one(2 * i + 1, keep_sum.at[i % 2])
+
+        def send_far(s, to):
+            state["far", s] = links.send(far_sum.at[s], half_land.at[kind, s], to)
+
+        def first_blocks():
+            if kind == 0:
+                for slot in range(2):
+                    row_load(0, far_blocks[slot], slot, early, 1).wait()
+                pair = []
+                for s in range(2):
+                    combine_late(0, s)
+                    pair.append(links.send(give.at[0, s], mate_sum.at[s], to_mate))
+                gifts.append(pair)
+                for s in range(2):
+                    combine_late(1, s)
+                settle_rows(0)
+                row_load(kind, order[2], 0).start()
+                for s, to in ((0, to_right), (1, to_left)):
+                    links.arrive(pair[s], mate_sum.at[s], to_mate)
+                    far_sum[s] += mate_sum[s]
+                    send_far(s, to)
+            else:
+                settle_rows(1)
+                row_load(kind, order[0], 0).start()
+                give_block(0)
+                for s in range(2):
+                    links.finish(y_sum["far", s])
+                one(1, far_sum)
+
+        def first_sum():
+            links.arrive(gifts[0], mate_land.at[kind, 0], to_mate)
+            copy = pltpu.make_async_copy(mate_land.at[kind, 0], mate_sum, sum_sem.at[0])
+            copy.start()
+            copy.wait()
+            for s, to in ((0, to_right), (1, to_left)):
+                far_sum[s] += mate_sum[s]
+                send_far(s, to)
 
         def add_mate(i):
             links.arrive(gifts[i], mate_land.at[kind, i], to_mate)
@@ -422,37 +536,47 @@
 
         def send_sum(i):
             writes[i].wait()
-            if i == 0:
-                state["far right"] = links.send(sums.at[kind, 0, 0], half_land.at[kind, 0], to_right)
-                state["far left"] = links.send(sums.at[kind, 0, 1], half_land.at[kind, 1], to_left)
-            elif i == 1:
+            if i == 1:
                 state["right"] = links.send(sums.at[kind, 1, 1], last_land.at[kind, 0, 1], to_right)
             elif i == 2:
                 state["left"] = links.send(sums.at[kind, 2, 0], last_land.at[kind, 1, 0], to_left)
 
-        give_block(0)
-        own_block(0)
-        give_block(1)
-        add_mate(0)
-        send_sum(0)
-        own_block(1)
-        give_block(2)
-        add_mate(1)
-        own_block(2)
-        send_sum(1)
-        give_block(3)
-        add_mate(2)
-        own_block(3)
-        send_sum(2)
-        add_mate(3)
-        send_sum(3)
+        with jax.named_scope("first_blocks"):
+            first_blocks()
+        with jax.named_scope("give_block_1"):
+            give_block(1)
+        if kind == 1:
+            with jax.named_scope("first_sum"):
+                first_sum()
+        with jax.named_scope("own_block_1"):
+            own_block(1)
+        with jax.named_scope("give_block_2"):
+            give_block(2)
+        with jax.named_scope("add_mate_1"):
+            add_mate(1)
+        with jax.named_scope("own_block_2"):
+            own_block(2)
+        with jax.named_scope("send_sum_1"):
+            send_sum(1)
+        with jax.named_scope("give_block_3"):
+            give_block(3)
+        with jax.named_scope("add_mate_2"):
+            add_mate(2)
+        with jax.named_scope("own_block_3"):
+            own_block(3)
+        with jax.named_scope("send_sum_2"):
+            send_sum(2)
+        with jax.named_scope("add_mate_3"):
+            add_mate(3)
+        with jax.named_scope("send_sum_3"):
+            send_sum(3)
         links.finish(gifts[2])
         links.finish(gifts[3])
         return state
 
     def turn_sums(kind, state):
-        for s, key, to, back in ((0, "far right", to_right, to_right), (1, "far left", to_left, to_left)):
-            links.arrive(state[key], half_land.at[kind, s], back)
+        for s, to in ((0, to_right), (1, to_left)):
+            links.arrive(state["far", s], half_land.at[kind, s], to)
             tile = turn_sum.at[kind, s]
             a = pltpu.make_async_copy(sums.at[kind, 1 + s, s], tile, sum_sem.at[0])
             b = pltpu.make_async_copy(half_land.at[kind, s], mate_sum.at[s], sum_sem.at[1])
@@ -463,11 +587,41 @@
             turn_sum[kind, s] += mate_sum[s]
             state["turn", s] = links.send(tile, last_land.at[kind, s, s], to)
 
-    def sums_here(kind, state):
+    def direct_here(kind, state):
         links.arrive(state["right"], last_land.at[kind, 0, 1], to_right)
         links.arrive(state["left"], last_land.at[kind, 1, 0], to_left)
+
+    def turned_here(kind, state):
         links.arrive(state["turn", 0], last_land.at[kind, 0, 0], to_right)
         links.arrive(state["turn", 1], last_land.at[kind, 1, 1], to_left)
+
+    def add_direct(kind):
+        copies = [pltpu.make_async_copy(sums.at[kind, 3], keep_sum.at[0], sum_sem.at[0]),
+                  pltpu.make_async_copy(last_land.at[kind, 1, 0], mate_sum.at[0], sum_sem.at[1]),
+                  pltpu.make_async_copy(last_land.at[kind, 0, 1], mate_sum.at[1], sum_sem.at[2])]
+        for copy in copies:
+            copy.start()
+        for copy in copies:
+            copy.wait()
+        keep_sum[0] += mate_sum[...]
+
+    def finish_out():
+        add_direct(0)
+        copies = [pltpu.make_async_copy(last_land.at[0, s, s], mate_sum.at[s], sum_sem.at[s]) for s in range(2)]
+        for copy in copies:
+            copy.start()
+        for s in range(2):
+            copies[s].wait()
+            xb[0, 0, :, s * side : (s + 1) * side] = (keep_sum[0, s] + mate_sum[s]).astype(BF16)
+        copy = pltpu.make_async_copy(xb.at[0, 0], out, sum_sem.at[0])
+        copy.start()
+        copy.wait()
+
+    def fold_dx():
+        add_direct(1)
+        copy = pltpu.make_async_copy(keep_sum.at[0], sums.at[1, 3], sum_sem.at[0])
+        copy.start()
+        copy.wait()
 
     y_state = {}
     for way in (True, False):
@@ -485,75 +639,127 @@
     for copy in stow:
         copy.start()
     earlier[...] = earlier_rows(earlier.shape[0])
-    acc13[...] = jnp.zeros_like(acc13)
-    acc2[...] = jnp.zeros_like(acc2)
+    with jax.named_scope("zeros"):
+        acc13[...] = jnp.zeros_like(acc13)
+        acc2[...] = jnp.zeros_like(acc2)
 
     def y_arrive(kind, way):
         block = all_refs[kind].at[ep, down if way else up]
         links.arrive(y_state[kind, way], block, to_up if way else to_down)
         return block
 
-    pass_on(0)
-    for way in (True, False):
-        for kind in kinds:
-            y_arrive(kind, way)
-    send_weights(0)
-    send_weights(1)
+    with jax.named_scope("pass_on_0"):
+        pass_on(0)
+    with jax.named_scope("y_arrive"):
+        for way in (True, False):
+            for kind in kinds:
+                y_arrive(kind, way)
+    with jax.named_scope("send_weights_0"):
+        send_weights(0)
+    with jax.named_scope("send_weights_1"):
+        send_weights(1)
     for g in (1, 2):
         states.append(spread(groups[g], [ref.at[ep, groups[g]] for ref in all_refs]))
-    share(0)
-    last(0)
+    with jax.named_scope("share_0"):
+        share(0)
+    with jax.named_scope("last_0"):
+        last(0)
     for copy in hold + stow:
         copy.wait()
-    from_mate(0)
+    with jax.named_scope("from_mate_0"):
+        from_mate(0)
     route_copy = pltpu.make_async_copy(r_all.at[:, tp], routes, row_sem.at[0])
     route_copy.start()
     route_copy.wait()
-    compute(tp, True)
-
-    pass_weights(0)
-    send_weights(2)
-    pass_on(1)
-    share(1)
-    pass_weights(1)
-    send_weights(3)
-    expert(0)
-    pass_on(2)
-    share(2)
-    pass_weights(2)
-    send_weights(4)
-    last(1)
-    from_mate(1)
-    expert(1)
-    last(2)
-    compute(groups[1], False)
-    pass_weights(3)
-    expert(2)
-    from_mate(2)
-    compute(groups[2], False)
-    pass_weights(4)
-    over_state = send_over()
-    expert(3)
-    have_weights(own - 1)
-    copies = fetch(own - 1)
-    forward(own - 1, copies)
-    y_sum = sum_up(0)
-    share_over(0)
-    backward(own - 1, copies)
-    dx_sum = sum_up(1)
-    turn_sums(0, y_sum)
-    share_over(1)
-    have_over(0)
-    have_over(1)
-    start_loads(over, 0)
-    half_group(over, 0, False, False)
-    share_over(2)
-    turn_sums(1, dx_sum)
-    share_over(3)
-    have_over(2)
-    have_over(3)
-    start_loads(over, 1)
-    half_group(over, 1, False, False)
+    with jax.named_scope("compute_tp_True"):
+        compute(tp, True)
+
+    with jax.named_scope("pass_weights_0"):
+        pass_weights(0)
+    with jax.named_scope("send_weights_2"):
+        send_weights(2)
+    with jax.named_scope("pass_on_1"):
+        pass_on(1)
+    with jax.named_scope("share_1"):
+        share(1)
+    with jax.named_scope("pass_weights_1"):
+        pass_weights(1)
+    with jax.named_scope("send_weights_3"):
+        send_weights(3)
+    with jax.named_scope("expert_0"):
+        expert(0)
+    with jax.named_scope("pass_on_2"):
+        pass_on(2)
+    with jax.named_scope("share_2"):
+        share(2)
+    with jax.named_scope("pass_weights_2"):
+        pass_weights(2)
+    with jax.named_scope("send_weights_4"):
+        send_weights(4)
+    with jax.named_scope("last_1"):
+        last(1)
+    with jax.named_scope("from_mate_1"):
+        from_mate(1)
+    with jax.named_scope("expert_1"):
+        expert(1)
+    with jax.named_scope("last_2"):
+        last(2)
+    with jax.named_scope("compute_groups_1_False"):
+        compute(groups[1], False)
+    with jax.named_scope("pass_weights_3"):
+        pass_weights(3)
+    with jax.named_scope("expert_2"):
+        expert(2)
+    with jax.named_scope("from_mate_2"):
+        from_mate(2)
+    with jax.named_scope("compute_groups_2_False"):
+        compute(groups[2], False)
+    with jax.named_scope("pass_weights_4"):
+        pass_weights(4)
+    with jax.named_scope("send_over_"):
+        over_state = send_over()
+    with jax.named_scope("combine_early"):
+        settle_rows(0)
+        combine_early()
+    with jax.named_scope("expert_3"):
+        expert(3)
+    with jax.named_scope("forward_early"):
+        load_next()
+        copies = forward_early(own - 1)
+    with jax.named_scope("have_weights_own_1"):
+        have_weights(own - 1)
+    with jax.named_scope("forward_late"):
+        forward_late(own - 1)
+    with jax.named_scope("sum_up_0"):
+        y_sum = sum_up(0)
+    with jax.named_scope("share_over_0"):
+        share_over(0)
+    with jax.named_scope("backward_own_1_copies"):
+        backward(own - 1, copies)
+    with jax.named_scope("sum_up_1"):
+        dx_sum = sum_up(1)
+    with jax.named_scope("turn_sums_0_y_sum"):
+        turn_sums(0, y_sum)
+    with jax.named_scope("share_over_1"):
+        share_over(1)
+    with jax.named_scope("have_over_1"):
+        have_over(0)
+        have_over(1)
+    with jax.named_scope("half_group_over_0"):
+        start_loads(over, 0)
+        half_group(over, 0, False, False)
+    with jax.named_scope("share_over_2"):
+        share_over(2)
+    with jax.named_scope("turn_sums_1_dx_sum"):
+        turn_sums(1, dx_sum)
+    with jax.named_scope("share_over_3"):
+        share_over(3)
+    with jax.named_scope("have_over_3"):
+        have_over(2)
+        have_over(3)
+    with jax.named_scope("half_group_over_1"):
+        start_loads(over, 1)
+        half_group(over, 1, False, False)
 
     def finish(e, carry):
         g_buf[0] = acc13[e, :width, :].T.astype(BF16)
@@ -567,32 +773,44 @@
             copy.wait()
         return carry
 
-    lax.fori_loop(0, own, finish, 0)
-    sums_here(0, y_sum)
-    sums_here(1, dx_sum)
-    links.drain()
-
-
-def layer(tokens, d_out, routes, w_one, w_three, w_two, ep_size, tp_size, cap):
+    with jax.named_scope("finish"):
+        lax.fori_loop(0, own, finish, 0)
+    with jax.named_scope("direct_here"):
+        direct_here(0, y_sum)
+        direct_here(1, dx_sum)
+    with jax.named_scope("fold_dx"):
+        fold_dx()
+    with jax.named_scope("turned_here_0"):
+        turned_here(0, y_sum)
+    with jax.named_scope("finish_out"):
+        finish_out()
+    with jax.named_scope("turned_here_1"):
+        turned_here(1, dx_sum)
+    with jax.named_scope("drain"):
+        links.drain()
+
+
+def layer(tokens, d_out, ids, gate_vals, w_one, w_three, w_two, ep_size, tp_size, cap):
     tok, model = tokens.shape
     own, width, _ = w_two.shape
     half = ep_size // 2
     rows = half * cap
     side = model // 2
-    vmem, hbm = pl.BlockSpec(memory_space=pltpu.VMEM), pl.BlockSpec(memory_space=pl.ANY)
+    hbm = pl.BlockSpec(memory_space=pl.ANY)
     shape = jax.ShapeDtypeStruct
+    routes = (2 * ids.shape[0], tok)
     copies = copy_count(own)
     slot_rows = ep_size * tp_size * cap * own
     vector = pltpu.VMEM
     dma = pltpu.SemaphoreType.DMA
     outs = pl.pallas_call(
         functools.partial(layer_kernel, own, cap, width),
-        in_specs=[vmem, vmem, vmem, hbm, hbm, hbm],
-        out_specs=[hbm] * 15,
+        in_specs=[hbm] * 7,
+        out_specs=[hbm] * 16,
         out_shape=[
             shape((ep_size, tp_size, tok, model), BF16),
             shape((ep_size, tp_size, tok, model), BF16),
-            shape((ep_size, tp_size) + routes.shape, F32),
+            shape((ep_size, tp_size) + routes, F32),
             shape((tp_size, own, model, 2 * width), BF16),
             shape((tp_size, own, width, model), BF16),
             shape((own, 2, rows, model), BF16),
@@ -602,17 +820,23 @@
             shape((2, 4, 2, tok, side), F32),
             shape((2, 2, tok, side), F32),
             shape((2, 2, 2, tok, side), F32),
+            shape((tok, model), BF16),
             shape((own, model, width), BF16),
             shape((own, model, width), BF16),
             shape((own, width, model), BF16),
         ],
         scratch_shapes=[
+            vector((tok, model), BF16),
+            vector((tok, model), BF16),
+            vector(routes, F32),
+            vector(ids.shape, jnp.int32),
+            vector((2, 3, own * cap, tok), BF16),
             vector((own, model, 2 * width), BF16),
             vector((own, width, model), BF16),
             vector((2, half // 2, tok, model), BF16),
             vector((2, half // 2, tok, model), BF16),
-            vector((2, half // 2) + routes.shape, F32),
-            vector((ep_size,) + routes.shape, F32),
+            vector((2, half // 2) + routes, F32),
+            vector((ep_size,) + routes, F32),
             vector((tok, tok), BF16),
             vector((own, rows, model), BF16),
             vector((own, rows, model), BF16),
@@ -631,10 +855,11 @@
             vector((2, 2, tok, side), F32),
             vector((2, 2, tok, side), F32),
             vector((2, tok, side), F32),
+            vector((2, tok, side), F32),
             vector((2, 2, tok, side), F32),
             dma((copies,)),
             dma((copies,)),
-            dma((3,)),
+            dma((4,)),
             dma((3, 2)),
             dma((3,)),
             dma((2,)),
@@ -651,28 +876,25 @@
             transcendentals=0,
         ),
         name="layer",
-    )(tokens, d_out, routes, w_one, w_three, w_two)
-    return outs[8], outs[11], outs[12:]
-
-
-def result_kernel(sums, last_land, g1, g3, g2, out, dx, o1, o3, o2, parts, rows, b1, b3, b2, in_sem, out_sem):
-    grads = ((g1, b1, o1), (g3, b3, o3), (g2, b2, o2))
-    takes = [pltpu.make_async_copy(src, buf, in_sem.at[k]) for k, (src, buf, _) in enumerate(grads)]
-    terms = [[pltpu.make_async_copy(sums.at[kind, 3], parts.at[kind, 2], in_sem.at[3 + kind]),
-              pltpu.make_async_copy(last_land.at[kind], parts.at[kind, pl.ds(0, 2)], in_sem.at[5 + kind])] for kind in range(2)]
-    for copy in terms[0] + terms[1] + takes:
+    )(tokens, d_out, ids, gate_vals, w_one, w_three, w_two)
+    return outs[8], outs[11], outs[12], outs[13:]
+
+
+def result_kernel(sums, last_land, rows_in, g1, g3, g2, out, dx, o1, o3, o2, parts, rows, row_buf, b1, b3, b2, in_sem, out_sem):
+    moves = ((g1, b1, o1), (g3, b3, o3), (g2, b2, o2), (rows_in, row_buf, out))
+    takes = [pltpu.make_async_copy(src, buf, in_sem.at[k]) for k, (src, buf, _) in enumerate(moves)]
+    terms = [pltpu.make_async_copy(sums.at[1, 3], parts.at[0], in_sem.at[4])]
+    terms += [pltpu.make_async_copy(last_land.at[1, s, s], parts.at[1, s], in_sem.at[5 + s]) for s in range(2)]
+    for copy in terms + takes:
         copy.start()
-    puts = []
-    side = parts.shape[4]
-    for kind, to in ((0, out), (1, dx)):
-        for copy in terms[kind]:
-            copy.wait()
-        for s in range(2):
-            total = parts[kind, 2, s] + (parts[kind, 0, s] + parts[kind, 1, s])
-            rows[kind, :, s * side : (s + 1) * side] = total.astype(BF16)
-        puts.append(pltpu.make_async_copy(rows.at[kind], to, out_sem.at[3 + kind]))
-        puts[-1].start()
-    for k, (take, (_, buf, to)) in enumerate(zip(takes, grads)):
+    for copy in terms:
+        copy.wait()
+    side = parts.shape[3]
+    for s in range(2):
+        rows[:, s * side : (s + 1) * side] = (parts[0, s] + parts[1, s]).astype(BF16)
+    puts = [pltpu.make_async_copy(rows, dx, out_sem.at[4])]
+    puts[0].start()
+    for k, (take, (_, buf, to)) in enumerate(zip(takes, moves)):
         take.wait()
         puts.append(pltpu.make_async_copy(buf, to, out_sem.at[k]))
         puts[-1].start()
@@ -680,21 +902,22 @@
         copy.wait()
 
 
-def results(sums, last_land, grads):
+def results(sums, last_land, out, grads):
     _, _, _, tok, side = sums.shape
     hbm = pl.BlockSpec(memory_space=pl.ANY)
     row = jax.ShapeDtypeStruct((tok, 2 * side), BF16)
+    rows = pltpu.VMEM((tok, 2 * side), BF16)
     return pl.pallas_call(
         result_kernel,
-        in_specs=[hbm] * 5,
+        in_specs=[hbm] * 6,
         out_specs=[hbm] * 5,
         out_shape=[row, row] + [jax.ShapeDtypeStruct(g.shape, g.dtype) for g in grads],
-        scratch_shapes=[pltpu.VMEM((2, 3, 2, tok, side), F32), pltpu.VMEM((2, tok, 2 * side), BF16)]
+        scratch_shapes=[pltpu.VMEM((2, 2, tok, side), F32), rows, rows]
         + [pltpu.VMEM(g.shape, g.dtype) for g in grads]
         + [pltpu.SemaphoreType.DMA((7,)), pltpu.SemaphoreType.DMA((5,))],
         compiler_params=pltpu.CompilerParams(vmem_limit_bytes=VMEM_LIMIT),
         name="results",
-    )(sums, last_land, *grads)
+    )(sums, last_land, out, *grads)
 
 
 def solution(mesh):
@@ -707,9 +930,8 @@
 
     def local_step(tokens, expert_ids, gate_vals, w_one, w_three, w_two, d_out):
         cap = slot_count(expert_ids.shape[1], tokens.shape[0], w_one.shape[0] * ep_size)
-        routes = jnp.concatenate([expert_ids.T.astype(F32), gate_vals.T], axis=0)
-        sums, last_land, grads = layer(tokens, d_out, routes, w_one, w_three, w_two, ep_size, tp_size, cap)
-        return tuple(results(sums, last_land, grads))
+        sums, last_land, out, grads = layer(tokens, d_out, expert_ids.T, gate_vals.T, w_one, w_three, w_two, ep_size, tp_size, cap)
+        return tuple(results(sums, last_land, out, grads))
 
     return jax.shard_map(local_step, mesh=mesh,
                          in_specs=(row_spec, row_spec, row_spec, col_spec, col_spec, down_spec, row_spec),

time: 370 us -> 359 us (0.970)
  Pallas kernels: 367 us -> 358 us
    pallas_call x1, Pallas kernels: 359 us -> 351 us  [layer(): pl.pallas_call(functools.partial(layer_kernel, own, cap, width), in_specs...]
where the time goes in v5:
time: 359 us
  Pallas kernels  358 us (100%)
    pallas_call x1, Pallas kernels, layer(): pl.pallas_call(functools.partial(layer_kernel, own, cap, width), in_specs...  351 us

profile of v5, /device:TPU:97, one launch (start us, length us, event | category | flops | bytes accessed | tf_op | source)
XLA Modules:
  0.0 358.8 jit_solution(4655249465547756438)
XLA Ops:
  0.6 351.4 %layer.1 = (bf16[8,4,256,1536]{3,2,1,0:T(8,128)(2,1)}, bf16[8,4,256,1536]{3,2,1,0:T(8,128)(2,1)}, f32[8,4,16,256]{3,2,1,0:T(8,128)}, bf16[4,5,1536,256]{3,2,1,0:...) custom-call(bf16[256,1536]{1,0:T(8,128)(2,1)} %tokens.1, ...), custom_call_target="tpu_custom_call" | custom-call | flops 64424509440 | bytes 50331648 | tf_op jit(solution)/shard_map/layer/pallas_call | solution.py:806
  352.0 6.6 %results.1 = (bf16[256,1536]{1,0:T(8,128)(2,1)}, bf16[256,1536]{1,0:T(8,128)(2,1)}, bf16[5,1536,128]{2,1,0:T(8,128)(2,1)}, bf16[5,1536,128]{2,1,0:T(8,128)(2,1)}, bf16[5,128,1536]{2,1,0:T(8,128)(2,1)}) custom-call(f32[2,4,2,256,768]{4,3,2,1,0:T(8,128)} %get-tuple-element.11.sums, f32[2,2,2,256,768]{4,3,2,1,0:T(8,128)} %get-tuple-element.12.last_land, ...), custom_call_target="tpu_custom_call" | custom-call | tf_op jit(solution)/shard_map/results/pallas_call | solution.py:910
